TPU v7x, 256 devices: a whole 4x4x8 slice. The times are simulated.
256 devices in a mesh: nodes: 64 (over z, x, core), heads: 4 (over y).
Axes of the slice: x: 4, y: 4, z: 8, core: 2. Of those that a mesh axis runs over, the one named last changes fastest.
Arguments:
- nodes_in: bfloat16 [32768, 1024], P('nodes', 'heads'), may hold values from -6 to 6
- local_gain: float32 [1024], replicated, may hold values from 0.5 to 1.5
- neighbour_query_key_value: bfloat16 [3, 1024, 1024], P(None, None, 'heads'), may hold values from -0.25 to 0.25
- local_out: bfloat16 [1024, 1024], P('heads'), may hold values from -0.1875 to 0.1875
- global_gain: float32 [1024], replicated, may hold values from 0.5 to 1.5
- global_qkv: bfloat16 [3, 1024, 1024], P(None, None, 'heads'), may hold values from -0.1875 to 0.1875
- global_out: bfloat16 [1024, 1024], P('heads'), may hold values from -1.875 to 1.875
- feature_map: bfloat16 [16, 64, 128], P('heads'), may hold values from -5 to 5
- neighbour_count: int32 [256], P('nodes'), may hold values from 1 to 8
- neighbour_blocks: int32 [256, 8], P('nodes'), may hold values from 0 to 255, as said below
- metis_order: int32 [256], P('nodes'), may hold values from 0 to 255, as said below
- hashed_order: int32 [256], P('nodes'), may hold values from 0 to 255, as said below
Outputs:
- output: bfloat16 [32768, 1024], P('nodes', 'heads')
Inputs may be any that keep to these rules, and one draw needn't show every extreme that they name: `neighbour_blocks`: entry 0 of block b's list is b itself; every entry lies within 2 blocks of the aligned group of 4 blocks that holds b, inside the graph; entries from neighbour_count on are unused; entries may repeat. `metis_order`: A permutation of the block ids. `hashed_order`: A permutation of the block ids. The blocks at the 4 METIS positions of aligned group g go to the aligned groups of 4 hashed positions numbered (g + k * 16) modulo 64 for k = 0 to 3, exactly 1 of them to each; which block goes to which of these groups, and to which position in it, is drawn.
All inputs are finite; a program needn't handle non-finite values.
Results may differ from a plain program's by a relative error of at most 0.015.
Values may be sent and summed in bfloat16 or wider, within the bound.
No kernel may reach another device: no remote copies, remote signals or barrier semaphores. Data moves between devices by JAX's collectives and lax.ppermute only.
A program may use at most 64 MiB of HBM per device.

v0:
```python
import jax
import jax.numpy as jnp
from jax import lax
from jax.experimental import pallas as pl
from jax.experimental.pallas import tpu as pltpu
from jax.sharding import Mesh, PartitionSpec as P

D = 1024
HD = 64
FEAT = 128
BLOCK = 128
HALO_BLK = 2
PEERS = 4
COLS = D // PEERS
EPSILON = 1e-06
SUM_ROWS = 144
F32 = jnp.float32
BF16 = jnp.bfloat16


def vmem():
    return pl.BlockSpec(memory_space=pltpu.VMEM)


def smem():
    return pl.BlockSpec(memory_space=pltpu.SMEM)


def shifted(value, axis, steps):
    count = lax.axis_size(axis)
    return lax.ppermute(value, axis, [(i, (i + steps) % count) for i in range(count)])


def flipped(value, axis, mask):
    count = lax.axis_size(axis)
    return lax.ppermute(value, axis, [(i, i ^ mask) for i in range(count)])


def dot(a, b):
    return jnp.dot(a, b, preferred_element_type=F32)


def dot_t(a, b):
    return lax.dot_general(a, b, (((1,), (1,)), ((), ())), preferred_element_type=F32)


def dot_rows(a, b):
    return lax.dot_general(a, b, (((0,), (0,)), ((), ())), preferred_element_type=F32)


def norm_rows(scaled, part, gain, y):
    for r in range(0, scaled.shape[0], BLOCK):
        places = [pl.multiple_of(lax.rem(y + PEERS - k, PEERS) * COLS, COLS) for k in range(PEERS)]
        floats = [part(k, r, at) for k, at in enumerate(places)]
        total = sum(jnp.sum(f * f, axis=-1, keepdims=True) for f in floats)
        inverse = lax.rsqrt(total * (1.0 / D) + EPSILON)
        for f, at in zip(floats, places):
            line = gain[:, pl.ds(at, COLS)]
            scaled[r : r + BLOCK, pl.ds(at, COLS)] = (f * inverse * line).astype(BF16)


def preload_kernel(c_ref, x_far, gain_far, w_far, out_far, x, gain, w, cut, sems):
    at = pl.multiple_of(c_ref[0] * (D // 2), D // 2)
    pairs = ((out_far.at[:, pl.ds(at, D // 2)], cut), (x_far, x), (gain_far, gain), (w_far, w))
    copies = [pltpu.make_async_copy(a, b, sems.at[i]) for i, (a, b) in enumerate(pairs)]
    for copy in copies:
        copy.start()
    for copy in copies:
        copy.wait()


def qkv_kernel(y_ref, x0, x1, x2, x3, gain, w, q, low, high, scaled):
    parts = (x0, x1, x2, x3)
    norm_rows(scaled, lambda k, r, at: parts[k][r : r + BLOCK, :].astype(F32), gain, y_ref[0])
    rows = scaled[...]
    half = rows.shape[0] // 2
    for t in (1, 2):
        out = dot(rows, w[t]).astype(BF16)
        low[t - 1] = out[:half]
        high[t - 1] = out[half:]
    q[...] = (dot(rows, w[0]).astype(BF16).astype(F32) * HD**-0.5).astype(BF16)


def head_masks(rows, width):
    lane = lax.broadcasted_iota(jnp.int32, (rows, width), 1)
    return [(lane // HD) == h for h in range(width // HD)]


def attention_kernel(q, before, low, high, after, bias, mixed):
    keys = [part[0] for part in (before, low, high, after)]
    values = [part[1] for part in (before, low, high, after)]
    width = q.shape[1]
    heads = width // HD
    masks = head_masks(BLOCK, width)
    span = keys[0].shape[0]
    for b in range(q.shape[0] // BLOCK):
        rows = q[b * BLOCK : (b + 1) * BLOCK, :].astype(F32)
        stacked = jnp.concatenate([jnp.where(m, rows, 0.0).astype(BF16) for m in masks], axis=0)
        add = bias[b]
        scores = [
            dot_t(stacked, k) + add[:, j * span : (j + 1) * span] for j, k in enumerate(keys)
        ]
        top = jnp.max(
            jnp.maximum(jnp.maximum(scores[0], scores[1]), jnp.maximum(scores[2], scores[3])),
            axis=-1,
            keepdims=True,
        )
        expo = [jnp.exp(s - top) for s in scores]
        totals = jnp.sum((expo[0] + expo[1]) + (expo[2] + expo[3]), axis=-1, keepdims=True)
        acc = sum(dot(e.astype(BF16), v) for e, v in zip(expo, values))
        acc = acc / totals
        picked = acc[:BLOCK]
        for h in range(1, heads):
            picked = jnp.where(masks[h], acc[h * BLOCK : (h + 1) * BLOCK], picked)
        mixed[b * BLOCK : (b + 1) * BLOCK, :] = picked.astype(BF16)


def project(y, mixed, w, outs):
    rows = mixed[...]
    for k, out in enumerate(outs):
        at = pl.multiple_of(lax.rem(y + k, PEERS) * COLS, COLS)
        out[...] = dot(rows, w[:, pl.ds(at, COLS)]).astype(BF16).astype(out.dtype)


def spread_features(features, spread):
    spread[...] = jnp.zeros(spread.shape, spread.dtype)
    for h in range(features.shape[0]):
        spread[h * HD : (h + 1) * HD, h * FEAT : (h + 1) * FEAT] = features[h]


def feature_rows(rows, spread):
    angles = dot(rows, spread) * HD**-0.5
    return jnp.where(angles > 0, angles + 1.0, jnp.exp(jnp.minimum(angles, 0.0))).astype(BF16)


def global_kernel(
    y_ref, c_ref, pick, x0, x1, x2, x3, m0, m1, m2, m3, w_own, a1, a2, a3, b1, b2, b3, gain, w, features,
    s0, s1, s2, s3, u0, u1, u2, u3, summary, local, scaled, spread, queries, hidden,
):
    c = c_ref[0]
    wide = D // 2
    for side, given in ((c, (a1, a2, a3)), (1 - c, (b1, b2, b3))):
        at = pl.multiple_of(side * wide, wide)
        out = dot(m0[...], w_own[:, pl.ds(at, wide)])
        for m, part in zip((m1, m2, m3), given):
            out = out + dot(m[...], part[...])
        local[:, pl.ds(at, wide)] = out
    parts = (x0, x1, x2, x3)

    def hidden_rows(k, r, at):
        value = parts[k][r : r + BLOCK, :].astype(F32) + local[r : r + BLOCK, pl.ds(at, COLS)]
        value = value.astype(BF16)
        if k == 0:
            hidden[r : r + BLOCK, :] = value
        return value.astype(F32)

    norm_rows(scaled, hidden_rows, gain, y_ref[0])
    spread_features(features, spread)
    rows = scaled[...]
    gk = dot(rows, w[1]).astype(BF16)
    gv = dot(rows, w[2]).astype(BF16)
    phi = feature_rows(gk, spread[...])
    sums = dot_rows(phi, gv)
    lane = lax.broadcasted_iota(jnp.int32, (FEAT, 2 * HD), 1)
    for pair in range(2):
        a, b = 2 * pair, 2 * pair + 1
        at = pair * 2 * HD
        left = sums[a * FEAT : (a + 1) * FEAT, at : at + 2 * HD]
        right = sums[b * FEAT : (b + 1) * FEAT, at : at + 2 * HD]
        summary[0:FEAT, at : at + 2 * HD] = jnp.where(lane < HD, left, right).astype(BF16)
    totals = jnp.sum(phi.astype(F32), axis=0, keepdims=True)
    pads = [jnp.zeros((1, FEAT), F32)] * (SUM_ROWS - FEAT - PEERS)
    tail = jnp.concatenate([totals[:, h * FEAT : (h + 1) * FEAT] for h in range(PEERS)] + pads, axis=0)
    summary[FEAT:SUM_ROWS, 0:FEAT] = tail.astype(BF16)
    summary[FEAT:SUM_ROWS, FEAT : 2 * FEAT] = jnp.zeros((SUM_ROWS - FEAT, FEAT), BF16)
    queries[...] = dot(rows, w[0]).astype(BF16)
    for s, (send, keep) in enumerate(((s0, u0), (s1, u1), (s2, u2), (s3, u3))):
        at = pl.multiple_of(pick[s] * BLOCK, BLOCK)
        send[...] = queries[pl.ds(at, BLOCK), :]
        keep[...] = hidden[pl.ds(at, BLOCK), :]


def final_kernel(
    y_ref, place, g0, g1, g2, g3, t0, t1, t2, t3, features, w, own, p1, p2, p3, rows, mixed, spread, table
):
    spread_features(features, spread)
    total = added(t0[...], t1[...], t2[...], t3[...])
    lane = lax.broadcasted_iota(jnp.int32, (FEAT, 2 * HD), 1)
    table[...] = jnp.zeros(table.shape, table.dtype)
    for h in range(PEERS):
        at = (h // 2) * 2 * HD
        mine = (lane // HD) == (h % 2)
        part = jnp.where(mine, total[0:FEAT, at : at + 2 * HD], 0.0)
        line = total[FEAT + h : FEAT + h + 1, 0:FEAT]
        column = jnp.transpose(jnp.broadcast_to(line, (FEAT, FEAT)))
        column = jnp.where(mine, column, 0.0)
        for n, value in enumerate((part, column)):
            top = value.astype(BF16)
            table[2 * n, h * FEAT : (h + 1) * FEAT, at : at + 2 * HD] = top
            table[2 * n + 1, h * FEAT : (h + 1) * FEAT, at : at + 2 * HD] = (
                value - top.astype(F32)
            ).astype(BF16)
    for s, got in enumerate((g0, g1, g2, g3)):
        at = pl.multiple_of(place[s] * BLOCK, BLOCK)
        rows[pl.ds(at, BLOCK), :] = got[...]
    phi = feature_rows(rows[...], spread[...])
    numerator = dot(phi, table[0]) + dot(phi, table[1])
    denominator = dot(phi, table[2]) + dot(phi, table[3])
    mixed[...] = (numerator / denominator).astype(BF16)
    project(y_ref[0], mixed, w, (own, p1, p2, p3))


def sum_kernel(place, own, p1, p2, p3, u0, u1, u2, u3, out):
    for s, keep in enumerate((u0, u1, u2, u3)):
        rows = pl.ds(pl.multiple_of(place[s] * BLOCK, BLOCK), BLOCK)
        parts = [part[rows, :].astype(F32) for part in (own, p1, p2, p3)]
        out[rows, :] = (keep[...].astype(F32) + sum(parts)).astype(BF16)


def call(kernel, outs, scratch=(), limit=24, far=()):
    def run(*args):
        specs = [smem() if a.dtype == jnp.int32 else vmem() for a in args]
        args = list(args)
        for i in far:
            specs[i] = pl.BlockSpec(memory_space=pltpu.HBM)
            args[i] = pltpu.with_memory_space_constraint(args[i], pltpu.HBM)
        return pl.pallas_call(
            kernel,
            in_specs=specs,
            out_specs=[vmem() for _ in outs],
            out_shape=[jax.ShapeDtypeStruct(s, d) for s, d in outs],
            scratch_shapes=[s if not isinstance(s, tuple) else pltpu.VMEM(*s) for s in scratch],
            compiler_params=pltpu.CompilerParams(vmem_limit_bytes=limit * 2**20),
        )(*args)

    return run


def added(*parts):
    return sum(p.astype(F32) for p in parts)


def body(
    nodes_in,
    local_gain,
    qkv,
    local_out,
    global_gain,
    global_qkv,
    global_out,
    feature_map,
    counts,
    neighbours,
    metis,
    hashed,
):
    nodes_axes = ("zq", "zr", "x", "c")
    devices = lax.axis_size(nodes_axes)
    device = lax.axis_index(nodes_axes)
    rows = nodes_in.shape[0]
    blocks = counts.shape[0]
    half = rows // 2
    y = lax.axis_index("y").astype(jnp.int32).reshape(1)
    core = lax.axis_index("c").astype(jnp.int32).reshape(1)
    gains = (local_gain.reshape(1, D), global_gain.reshape(1, D))

    inputs = [nodes_in] + [shifted(nodes_in, "y", k) for k in range(1, PEERS)]
    given = (nodes_in, gains[0], qkv, local_out)
    own_x, own_gain, qkv, mine = call(
        preload_kernel,
        [(g.shape, g.dtype) for g in given[:3]] + [((COLS, D // 2), BF16)],
        [pltpu.SemaphoreType.DMA((len(given),))],
        far=(1, 2, 3, 4),
    )(core, *given)
    ids = jnp.stack([metis, hashed])[None]
    ids = jnp.concatenate([ids, flipped(ids, "zq", 1)])
    ids = jnp.concatenate([ids, flipped(ids, "zq", 2)])
    mine = [shifted(mine, "y", k) for k in range(1, PEERS)]
    other = [shifted(m, "c", 1) for m in mine]
    order = jnp.arange(PEERS, dtype=jnp.int32)

    def where_in(wanted, lists):
        found = jnp.any(lists[:, None, :] == wanted[None, :, None], axis=2)
        return jnp.sum(jnp.where(found, order[None, :], 0), axis=1)

    pick = where_in(metis, ids[:, 1])
    place = where_in(hashed, ids[:, 0])

    window = blocks + 2 * HALO_BLK
    local_index = neighbours - (device * blocks - HALO_BLK)
    slots = jnp.arange(neighbours.shape[1], dtype=jnp.int32)
    hits = (local_index[:, :, None] == jnp.arange(window, dtype=jnp.int32)) & (
        slots[None, :, None] < counts[:, None, None]
    )
    times = jnp.sum(hits.astype(F32), axis=1)
    bias = jnp.where(times > 0, jnp.log(jnp.maximum(times, 1.0)), -1e30)
    bias = jnp.repeat(bias, BLOCK, axis=1).reshape(blocks, 1, window * BLOCK)

    pair = (2, half, COLS)
    q, low, high = call(
        qkv_kernel,
        [((rows, COLS), BF16), (pair, BF16), (pair, BF16)],
        [((rows, D), BF16)],
    )(y, own_x, *inputs[1:], own_gain, qkv)
    up = [(i, i + 1) for i in range(devices - 1)]
    before = lax.ppermute(high, nodes_axes, up)
    after = lax.ppermute(low, nodes_axes, [(j, i) for i, j in up])

    piece = ((rows, COLS), BF16)
    (mixed,) = call(attention_kernel, [piece])(q, before, low, high, after, bias)
    mixed = [mixed] + [shifted(mixed, "y", k) for k in range(1, PEERS)]

    block = ((BLOCK, COLS), BF16)
    *sends, summary = call(
        global_kernel,
        [block] * (2 * PEERS) + [((SUM_ROWS, COLS), BF16)],
        [((rows, D), F32), ((rows, D), BF16), ((COLS, PEERS * FEAT), BF16), piece, piece],
    )(y, core, pick, own_x, *inputs[1:], *mixed, local_out, *mine, *other, gains[1], global_qkv, feature_map)

    got = [sends[0]] + [flipped(sends[k], "zq", k) for k in range(1, PEERS)]
    kept = sends[PEERS:]
    kept = [kept[0]] + [flipped(kept[k], "zq", k) for k in range(1, PEERS)]
    summary = added(summary, shifted(summary, "c", 1)).astype(BF16)
    summary = added(summary, *[shifted(summary, "x", k) for k in range(1, 4)]).astype(BF16)
    summary = added(summary, shifted(summary, "zr", 1)).astype(BF16)
    parts = [summary] + [shifted(summary, "zq", k) for k in range(1, PEERS)]

    outs = call(
        final_kernel,
        [piece] * PEERS,
        [piece, piece, ((COLS, PEERS * FEAT), BF16), ((4, PEERS * FEAT, COLS), BF16)],
    )(y, place, *got, *parts, feature_map, global_out)
    outs = [outs[0]] + [shifted(p, "y", k) for k, p in enumerate(outs[1:], 1)]
    (result,) = call(sum_kernel, [piece])(place, *outs, *kept)
    return result


def solution(mesh):
    fine = Mesh(mesh.devices.reshape(4, 2, 4, 2, 4), ("zq", "zr", "x", "c", "y"))
    n = ("zq", "zr", "x", "c")
    in_specs = (
        P(n, "y"),
        P(),
        P(None, None, "y"),
        P("y", None),
        P(),
        P(None, None, "y"),
        P("y", None),
        P("y", None, None),
        P(n),
        P(n, None),
        P(n),
        P(n),
    )

    def step(*args):
        return body(*args)

    step = jax.shard_map(step, mesh=fine, in_specs=in_specs, out_specs=P(n, "y"), check_vma=False)
    return step
```

profile of v0, /device:TPU:32, one launch (start us, length us, event | category | flops | bytes accessed | tf_op | source)
XLA Modules:
  0.0 114.1 jit_solution(9835297406792499524)
XLA Ops:
  0.0 1.6 %collective-permute-start.2 = (bf16[512,256]{1,0:T(8,128)(2,1)}, bf16[512,256]{1,0:T(8,128)(2,1)S(1)}, u32[]{:S(2)}, u32[]{:S(2)}) collective-permute-start(bf16[512,256]{1,0:T(8,128)(2,1)} %x_far.1), channel_id=1, source_target_pairs={{0,1},{1,2},{2,3},{3,0},{4,5},{5,6},{6,7},{7,4},{8,9},{9,10},{10,1... | collective-permute-start | bytes 786440 | tf_op jit(solution)/shard_map/ppermute | solution.py:31
  1.6 1.7 %collective-permute-start.4 = (bf16[512,256]{1,0:T(8,128)(2,1)}, bf16[512,256]{1,0:T(8,128)(2,1)S(1)}, u32[]{:S(2)}, u32[]{:S(2)}) collective-permute-start(bf16[512,256]{1,0:T(8,128)(2,1)} %x_far.1), channel_id=1, source_target_pairs={{0,3},{1,0},{2,1},{3,2},{4,7},{5,4},{6,5},{7,6},{8,11},{9,8},{10,9... | collective-permute-start | bytes 786440 | tf_op jit(solution)/shard_map/ppermute | solution.py:31
  3.2 2.0 %collective-permute-start.3 = (bf16[512,256]{1,0:T(8,128)(2,1)}, bf16[512,256]{1,0:T(8,128)(2,1)S(1)}, u32[]{:S(2)}, u32[]{:S(2)}) collective-permute-start(bf16[512,256]{1,0:T(8,128)(2,1)} %x_far.1), channel_id=1, source_target_pairs={{0,2},{1,3},{2,0},{3,1},{4,6},{5,7},{6,4},{7,5},{8,10},{9,11},{10,... | collective-permute-start | bytes 786440 | tf_op jit(solution)/shard_map/ppermute | solution.py:31
  5.9 3.3 %collective-permute-start = (s32[1,2,4]{2,1,0:T(2,128)S(1)}, s32[1,2,4]{2,1,0:T(2,128)S(1)}, u32[]{:S(2)}, u32[]{:S(2)}) collective-permute-start(s32[1,2,4]{2,1,0:T(2,128)S(1)} %add_bitcast_fusion), channel_id=1, source_target_pairs={{0,64},{64,0},{128,192},{192,128},{1,65},{65,1},{129,193},{193,129... | collective-permute-start | bytes 104 | tf_op jit(solution)/shard_map/ppermute | solution.py:36
  9.2 1.6 %shard_map.118 = (bf16[512,256]{1,0:T(8,128)(2,1)S(1)}, f32[1,1024]{1,0:T(1,128)S(1)}, bf16[3,1024,256]{2,1,0:T(8,128)(2,1)S(1)}, bf16[256,512]{1,0:T(8,128)(2,1)S(1)}) custom-call(s32[1]{0:T(128)} %bitcast.5.c_ref, bf16[512,256]{1,0:T(8,128)(2,1)} %x_far.1, f32[1,1024]{1,0:T(1,128)} %bitcast.15, bf16[3,1024,256]{2,1,0:T(8,128)(2,1)} %w_far.1, ...), custom_call_target="tpu_custom_call" | custom-call | tf_op jit(solution)/shard_map/pallas_call | solution.py:227
  12.1 1.8 %collective-permute-start.11 = (bf16[256,512]{1,0:T(8,128)(2,1)S(1)}, bf16[256,512]{1,0:T(8,128)(2,1)S(1)}, u32[]{:S(2)}, u32[]{:S(2)}) collective-permute-start(bf16[256,512]{1,0:T(8,128)(2,1)S(1)} %get-tuple-element.31), channel_id=1, source_target_pairs={{0,2},{1,3},{2,0},{3,1},{4,6},{5,7},{6,4},{7,5},{8,10},{9,11},{10,... | collective-permute-start | bytes 786440 | tf_op jit(solution)/shard_map/ppermute | solution.py:31
  14.1 6.8 %collective-permute-start.1 = (s32[2,2,4]{2,1,0:T(2,128)S(1)}, s32[2,2,4]{2,1,0:T(2,128)S(1)}, u32[]{:S(2)}, u32[]{:S(2)}) collective-permute-start(s32[2,2,4]{2,1,0:T(2,128)S(1)} %pad_add_fusion.1), channel_id=1, source_target_pairs={{0,128},{64,192},{128,0},{192,64},{1,129},{65,193},{129,1},{193,65... | collective-permute-start | bytes 200 | tf_op jit(solution)/shard_map/ppermute | solution.py:36
  22.3 1.9 %collective-permute-start.5 = (bf16[2,256,256]{2,1,0:T(8,128)(2,1)S(1)}, bf16[2,256,256]{2,1,0:T(8,128)(2,1)S(1)}, u32[]{:S(2)}, u32[]{:S(2)}) collective-permute-start(bf16[2,256,256]{2,1,0:T(8,128)(2,1)S(1)} %get-tuple-element.29.high), channel_id=1, source_target_pairs={{0,4},{4,8},{8,12},{12,16},{16,20},{20,24},{24,28},{28,32},{32,36}... | collective-permute-start | bytes 786440 | tf_op jit(solution)/shard_map/ppermute | solution.py:306
  24.3 5.8 %collective-permute-start.6 = (bf16[2,256,256]{2,1,0:T(8,128)(2,1)S(1)}, bf16[2,256,256]{2,1,0:T(8,128)(2,1)S(1)}, u32[]{:S(2)}, u32[]{:S(2)}) collective-permute-start(bf16[2,256,256]{2,1,0:T(8,128)(2,1)S(1)} %get-tuple-element.30.low), channel_id=1, source_target_pairs={{4,0},{8,4},{12,8},{16,12},{20,16},{24,20},{28,24},{32,28},{36,32}... | collective-permute-start | bytes 786440 | tf_op jit(solution)/shard_map/ppermute | solution.py:307
  32.1 1.8 %collective-permute-done.6.after = bf16[2,256,256]{2,1,0:T(8,128)(2,1)S(1)} collective-permute-done((bf16[2,256,256]{2,1,0:T(8,128)(2,1)S(1)}, bf16[2,256,256]{2,1,0:T(8,128)(2,1)S(1)}, u32[]{:S(2)}, u32[]{:S(2)}) %collective-permute-start.6) | collective-permute-done | bytes 262176 | tf_op jit(solution)/shard_map/ppermute | solution.py:307
  34.0 3.7 %shard_map.120.m0 = bf16[512,256]{1,0:T(8,128)(2,1)S(1)} custom-call(bf16[512,256]{1,0:T(8,128)(2,1)S(1)} %get-tuple-element.28.q, bf16[2,256,256]{2,1,0:T(8,128)(2,1)S(1)} %collective-permute-done.5.before, bf16[2,256,256]{2,1,0:T(8,128)(2,1)S(1)} %get-tuple-element.30.low, bf16[2,256,256]{2,1,0:T(8,128)(2,1)S(1)} %get-tuple-element.29.high, ...), custom_call_target="tpu_custom_call" | custom-call | tf_op jit(solution)/shard_map/pallas_call | solution.py:227
  37.6 4.3 %collective-permute-start.9 = (bf16[512,256]{1,0:T(8,128)(2,1)S(1)}, bf16[512,256]{1,0:T(8,128)(2,1)S(1)}, u32[]{:S(2)}, u32[]{:S(2)}) collective-permute-start(bf16[512,256]{1,0:T(8,128)(2,1)S(1)} %shard_map.120.m0), channel_id=1, source_target_pairs={{0,3},{1,0},{2,1},{3,2},{4,7},{5,4},{6,5},{7,6},{8,11},{9,8},{10,9... | collective-permute-start | bytes 786440 | tf_op jit(solution)/shard_map/ppermute | solution.py:31
  42.0 4.9 %collective-permute-start.8 = (bf16[512,256]{1,0:T(8,128)(2,1)S(1)}, bf16[512,256]{1,0:T(8,128)(2,1)S(1)}, u32[]{:S(2)}, u32[]{:S(2)}) collective-permute-start(bf16[512,256]{1,0:T(8,128)(2,1)S(1)} %shard_map.120.m0), channel_id=1, source_target_pairs={{0,2},{1,3},{2,0},{3,1},{4,6},{5,7},{6,4},{7,5},{8,10},{9,11},{10,... | collective-permute-start | bytes 786440 | tf_op jit(solution)/shard_map/ppermute | solution.py:31
  47.3 4.7 %collective-permute-done.9.m3 = bf16[512,256]{1,0:T(8,128)(2,1)S(1)} collective-permute-done((bf16[512,256]{1,0:T(8,128)(2,1)S(1)}, bf16[512,256]{1,0:T(8,128)(2,1)S(1)}, u32[]{:S(2)}, u32[]{:S(2)}) %collective-permute-start.9) | collective-permute-done | bytes 262176 | tf_op jit(solution)/shard_map/ppermute | solution.py:31
  52.0 2.1 %collective-permute-done.8.m2 = bf16[512,256]{1,0:T(8,128)(2,1)S(1)} collective-permute-done((bf16[512,256]{1,0:T(8,128)(2,1)S(1)}, bf16[512,256]{1,0:T(8,128)(2,1)S(1)}, u32[]{:S(2)}, u32[]{:S(2)}) %collective-permute-start.8) | collective-permute-done | bytes 262176 | tf_op jit(solution)/shard_map/ppermute | solution.py:31
  54.1 4.3 %collective-permute-done.7.m1 = bf16[512,256]{1,0:T(8,128)(2,1)S(1)} collective-permute-done((bf16[512,256]{1,0:T(8,128)(2,1)S(1)}, bf16[512,256]{1,0:T(8,128)(2,1)S(1)}, u32[]{:S(2)}, u32[]{:S(2)}) %collective-permute-start.7) | collective-permute-done | bytes 262176 | tf_op jit(solution)/shard_map/ppermute | solution.py:31
  58.4 4.1 %shard_map.121 = (bf16[128,256]{1,0:T(8,128)(2,1)S(1)}, bf16[128,256]{1,0:T(8,128)(2,1)S(1)}, bf16[128,256]{1,0:T(8,128)(2,1)S(1)}, bf16[128,256]{1,0:T(8,128)(2...) custom-call(s32[1]{0:T(128)} %bitcast.4.y_ref, ...), custom_call_target="tpu_custom_call" | custom-call | tf_op jit(solution)/shard_map/pallas_call | solution.py:227
  68.6 3.4 %collective-permute-done.21 = bf16[144,256]{1,0:T(8,128)(2,1)S(1)} collective-permute-done((bf16[144,256]{1,0:T(8,128)(2,1)S(1)}, bf16[144,256]{1,0:T(8,128)(2,1)S(1)}, u32[]{:S(2)}, u32[]{:S(2)}) %collective-permute-start.21) | collective-permute-done | bytes 73760 | tf_op jit(solution)/shard_map/ppermute | solution.py:31
  74.1 1.6 %collective-permute-start.16 = (bf16[128,256]{1,0:T(8,128)(2,1)S(1)}, bf16[128,256]{1,0:T(8,128)(2,1)S(1)}, u32[]{:S(2)}, u32[]{:S(2)}) collective-permute-start(bf16[128,256]{1,0:T(8,128)(2,1)S(1)} %get-tuple-element.33), channel_id=1, source_target_pairs={{0,64},{64,0},{128,192},{192,128},{1,65},{65,1},{129,193},{193,129... | collective-permute-start | bytes 196616 | tf_op jit(solution)/shard_map/ppermute | solution.py:36
  75.6 2.8 %collective-permute-start.17 = (bf16[128,256]{1,0:T(8,128)(2,1)S(1)}, bf16[128,256]{1,0:T(8,128)(2,1)S(1)}, u32[]{:S(2)}, u32[]{:S(2)}) collective-permute-start(bf16[128,256]{1,0:T(8,128)(2,1)S(1)} %get-tuple-element.34), channel_id=1, source_target_pairs={{0,128},{64,192},{128,0},{192,64},{1,129},{65,193},{129,1},{193,65... | collective-permute-start | bytes 196616 | tf_op jit(solution)/shard_map/ppermute | solution.py:36
  78.4 2.2 %collective-permute-start.18 = (bf16[128,256]{1,0:T(8,128)(2,1)S(1)}, bf16[128,256]{1,0:T(8,128)(2,1)S(1)}, u32[]{:S(2)}, u32[]{:S(2)}) collective-permute-start(bf16[128,256]{1,0:T(8,128)(2,1)S(1)} %get-tuple-element.35), channel_id=1, source_target_pairs={{0,192},{64,128},{128,64},{192,0},{1,193},{65,129},{129,65},{193,1... | collective-permute-start | bytes 196616 | tf_op jit(solution)/shard_map/ppermute | solution.py:36
  80.7 2.0 %collective-permute-start.26 = (bf16[144,256]{1,0:T(8,128)(2,1)S(1)}, bf16[144,256]{1,0:T(8,128)(2,1)S(1)}, u32[]{:S(2)}, u32[]{:S(2)}) collective-permute-start(bf16[144,256]{1,0:T(8,128)(2,1)S(1)} %add_convert_fusion.t0), channel_id=1, source_target_pairs={{0,192},{64,0},{128,64},{192,128},{1,193},{65,1},{129,65},{193,129... | collective-permute-start | bytes 221192 | tf_op jit(solution)/shard_map/ppermute | solution.py:31
  82.7 3.1 %collective-permute-start.25 = (bf16[144,256]{1,0:T(8,128)(2,1)S(1)}, bf16[144,256]{1,0:T(8,128)(2,1)S(1)}, u32[]{:S(2)}, u32[]{:S(2)}) collective-permute-start(bf16[144,256]{1,0:T(8,128)(2,1)S(1)} %add_convert_fusion.t0), channel_id=1, source_target_pairs={{0,128},{64,192},{128,0},{192,64},{1,129},{65,193},{129,1},{193,65... | collective-permute-start | bytes 221192 | tf_op jit(solution)/shard_map/ppermute | solution.py:31
  88.1 3.9 %collective-permute-done.25.t2 = bf16[144,256]{1,0:T(8,128)(2,1)S(1)} collective-permute-done((bf16[144,256]{1,0:T(8,128)(2,1)S(1)}, bf16[144,256]{1,0:T(8,128)(2,1)S(1)}, u32[]{:S(2)}, u32[]{:S(2)}) %collective-permute-start.25) | collective-permute-done | bytes 73760 | tf_op jit(solution)/shard_map/ppermute | solution.py:31
  92.0 1.6 %collective-permute-done.24.t1 = bf16[144,256]{1,0:T(8,128)(2,1)S(1)} collective-permute-done((bf16[144,256]{1,0:T(8,128)(2,1)S(1)}, bf16[144,256]{1,0:T(8,128)(2,1)S(1)}, u32[]{:S(2)}, u32[]{:S(2)}) %collective-permute-start.24) | collective-permute-done | bytes 73760 | tf_op jit(solution)/shard_map/ppermute | solution.py:31
  93.6 2.0 %shard_map.122 = (bf16[512,256]{1,0:T(8,128)(2,1)S(1)}, bf16[512,256]{1,0:T(8,128)(2,1)S(1)}, bf16[512,256]{1,0:T(8,128)(2,1)S(1)}, bf16[512,256]{1,0:T(8,128)(2,1)S(1)}) custom-call(s32[1]{0:T(128)} %bitcast.4.y_ref, s32[4]{0:T(128)S(1)} %select_reduce_fusion.1.place, bf16[128,256]{1,0:T(8,128)(2,1)S(1)} %get-tuple-element.32.g0, ...), custom_call_target="tpu_custom_call" | custom-call | tf_op jit(solution)/shard_map/pallas_call | solution.py:227
  95.6 1.9 %collective-permute-start.27 = (bf16[512,256]{1,0:T(8,128)(2,1)S(1)}, bf16[512,256]{1,0:T(8,128)(2,1)S(1)}, u32[]{:S(2)}, u32[]{:S(2)}) collective-permute-start(bf16[512,256]{1,0:T(8,128)(2,1)S(1)} %get-tuple-element.38), channel_id=1, source_target_pairs={{0,1},{1,2},{2,3},{3,0},{4,5},{5,6},{6,7},{7,4},{8,9},{9,10},{10,1... | collective-permute-start | bytes 786440 | tf_op jit(solution)/shard_map/ppermute | solution.py:31
  97.7 2.6 %collective-permute-start.29 = (bf16[512,256]{1,0:T(8,128)(2,1)S(1)}, bf16[512,256]{1,0:T(8,128)(2,1)S(1)}, u32[]{:S(2)}, u32[]{:S(2)}) collective-permute-start(bf16[512,256]{1,0:T(8,128)(2,1)S(1)} %get-tuple-element.40), channel_id=1, source_target_pairs={{0,3},{1,0},{2,1},{3,2},{4,7},{5,4},{6,5},{7,6},{8,11},{9,8},{10,9... | collective-permute-start | bytes 786440 | tf_op jit(solution)/shard_map/ppermute | solution.py:31
  100.5 3.3 %collective-permute-start.31 = (bf16[128,256]{1,0:T(8,128)(2,1)S(1)}, bf16[128,256]{1,0:T(8,128)(2,1)S(1)}, u32[]{:S(2)}, u32[]{:S(2)}) collective-permute-start(bf16[128,256]{1,0:T(8,128)(2,1)S(1)} %get-tuple-element.43), channel_id=1, source_target_pairs={{0,128},{64,192},{128,0},{192,64},{1,129},{65,193},{129,1},{193,65... | collective-permute-start | bytes 196616 | tf_op jit(solution)/shard_map/ppermute | solution.py:36
  103.8 2.5 %collective-permute-done.30.u1 = bf16[128,256]{1,0:T(8,128)(2,1)S(1)} collective-permute-done((bf16[128,256]{1,0:T(8,128)(2,1)S(1)}, bf16[128,256]{1,0:T(8,128)(2,1)S(1)}, u32[]{:S(2)}, u32[]{:S(2)}) %collective-permute-start.30) | collective-permute-done | bytes 65568 | tf_op jit(solution)/shard_map/ppermute | solution.py:36
  106.8 2.5 %collective-permute-done.31.u2 = bf16[128,256]{1,0:T(8,128)(2,1)S(1)} collective-permute-done((bf16[128,256]{1,0:T(8,128)(2,1)S(1)}, bf16[128,256]{1,0:T(8,128)(2,1)S(1)}, u32[]{:S(2)}, u32[]{:S(2)}) %collective-permute-start.31) | collective-permute-done | bytes 65568 | tf_op jit(solution)/shard_map/ppermute | solution.py:36
  109.3 3.4 %collective-permute-done.32.u3 = bf16[128,256]{1,0:T(8,128)(2,1)S(1)} collective-permute-done((bf16[128,256]{1,0:T(8,128)(2,1)S(1)}, bf16[128,256]{1,0:T(8,128)(2,1)S(1)}, u32[]{:S(2)}, u32[]{:S(2)}) %collective-permute-start.32) | collective-permute-done | bytes 65568 | tf_op jit(solution)/shard_map/ppermute | solution.py:36
  (74 shorter events, 19.0 us)
Async XLA Ops:
  0.0 13.9 %collective-permute-start.2 = (bf16[512,256]{1,0:T(8,128)(2,1)}, bf16[512,256]{1,0:T(8,128)(2,1)S(1)}, u32[]{:S(2)}, u32[]{:S(2)}) collective-permute-start(bf16[512,256]{1,0:T(8,128)(2,1)} %x_far.1), channel_id=1, source_target_pairs={{0,1},{1,2},{2,3},{3,0},{4,5},{5,6},{6,7},{7,4},{8,9},{9,10},{10,1... | collective-permute-start | bytes 786440 | tf_op jit(solution)/shard_map/ppermute | solution.py:31
  1.6 12.6 %collective-permute-start.4 = (bf16[512,256]{1,0:T(8,128)(2,1)}, bf16[512,256]{1,0:T(8,128)(2,1)S(1)}, u32[]{:S(2)}, u32[]{:S(2)}) collective-permute-start(bf16[512,256]{1,0:T(8,128)(2,1)} %x_far.1), channel_id=1, source_target_pairs={{0,3},{1,0},{2,1},{3,2},{4,7},{5,4},{6,5},{7,6},{8,11},{9,8},{10,9... | collective-permute-start | bytes 786440 | tf_op jit(solution)/shard_map/ppermute | solution.py:31
  3.2 17.7 %collective-permute-start.3 = (bf16[512,256]{1,0:T(8,128)(2,1)}, bf16[512,256]{1,0:T(8,128)(2,1)S(1)}, u32[]{:S(2)}, u32[]{:S(2)}) collective-permute-start(bf16[512,256]{1,0:T(8,128)(2,1)} %x_far.1), channel_id=1, source_target_pairs={{0,2},{1,3},{2,0},{3,1},{4,6},{5,7},{6,4},{7,5},{8,10},{9,11},{10,... | collective-permute-start | bytes 786440 | tf_op jit(solution)/shard_map/ppermute | solution.py:31
  5.9 6.2 %collective-permute-start = (s32[1,2,4]{2,1,0:T(2,128)S(1)}, s32[1,2,4]{2,1,0:T(2,128)S(1)}, u32[]{:S(2)}, u32[]{:S(2)}) collective-permute-start(s32[1,2,4]{2,1,0:T(2,128)S(1)} %add_bitcast_fusion), channel_id=1, source_target_pairs={{0,64},{64,0},{128,192},{192,128},{1,65},{65,1},{129,193},{193,129... | collective-permute-start | bytes 104 | tf_op jit(solution)/shard_map/ppermute | solution.py:36
  10.8 19.2 %collective-permute-start.12 = (bf16[256,512]{1,0:T(8,128)(2,1)S(1)}, bf16[256,512]{1,0:T(8,128)(2,1)S(1)}, u32[]{:S(2)}, u32[]{:S(2)}) collective-permute-start(bf16[256,512]{1,0:T(8,128)(2,1)S(1)} %get-tuple-element.31), channel_id=1, source_target_pairs={{0,3},{1,0},{2,1},{3,2},{4,7},{5,4},{6,5},{7,6},{8,11},{9,8},{10,9... | collective-permute-start | bytes 786440 | tf_op jit(solution)/shard_map/ppermute | solution.py:31
  12.1 18.1 %collective-permute-start.11 = (bf16[256,512]{1,0:T(8,128)(2,1)S(1)}, bf16[256,512]{1,0:T(8,128)(2,1)S(1)}, u32[]{:S(2)}, u32[]{:S(2)}) collective-permute-start(bf16[256,512]{1,0:T(8,128)(2,1)S(1)} %get-tuple-element.31), channel_id=1, source_target_pairs={{0,2},{1,3},{2,0},{3,1},{4,6},{5,7},{6,4},{7,5},{8,10},{9,11},{10,... | collective-permute-start | bytes 786440 | tf_op jit(solution)/shard_map/ppermute | solution.py:31
  13.9 16.8 %collective-permute-start.10 = (bf16[256,512]{1,0:T(8,128)(2,1)S(1)}, bf16[256,512]{1,0:T(8,128)(2,1)S(1)}, u32[]{:S(2)}, u32[]{:S(2)}) collective-permute-start(bf16[256,512]{1,0:T(8,128)(2,1)S(1)} %get-tuple-element.31), channel_id=1, source_target_pairs={{0,1},{1,2},{2,3},{3,0},{4,5},{5,6},{6,7},{7,4},{8,9},{9,10},{10,1... | collective-permute-start | bytes 786440 | tf_op jit(solution)/shard_map/ppermute | solution.py:31
  14.1 10.1 %collective-permute-start.1 = (s32[2,2,4]{2,1,0:T(2,128)S(1)}, s32[2,2,4]{2,1,0:T(2,128)S(1)}, u32[]{:S(2)}, u32[]{:S(2)}) collective-permute-start(s32[2,2,4]{2,1,0:T(2,128)S(1)} %pad_add_fusion.1), channel_id=1, source_target_pairs={{0,128},{64,192},{128,0},{192,64},{1,129},{65,193},{129,1},{193,65... | collective-permute-start | bytes 200 | tf_op jit(solution)/shard_map/ppermute | solution.py:36
  22.3 9.8 %collective-permute-start.5 = (bf16[2,256,256]{2,1,0:T(8,128)(2,1)S(1)}, bf16[2,256,256]{2,1,0:T(8,128)(2,1)S(1)}, u32[]{:S(2)}, u32[]{:S(2)}) collective-permute-start(bf16[2,256,256]{2,1,0:T(8,128)(2,1)S(1)} %get-tuple-element.29.high), channel_id=1, source_target_pairs={{0,4},{4,8},{8,12},{12,16},{16,20},{20,24},{24,28},{28,32},{32,36}... | collective-permute-start | bytes 786440 | tf_op jit(solution)/shard_map/ppermute | solution.py:306
  24.3 9.6 %collective-permute-start.6 = (bf16[2,256,256]{2,1,0:T(8,128)(2,1)S(1)}, bf16[2,256,256]{2,1,0:T(8,128)(2,1)S(1)}, u32[]{:S(2)}, u32[]{:S(2)}) collective-permute-start(bf16[2,256,256]{2,1,0:T(8,128)(2,1)S(1)} %get-tuple-element.30.low), channel_id=1, source_target_pairs={{4,0},{8,4},{12,8},{16,12},{20,16},{24,20},{28,24},{32,28},{36,32}... | collective-permute-start | bytes 786440 | tf_op jit(solution)/shard_map/ppermute | solution.py:307
  30.1 16.9 %collective-permute-start.15 = (bf16[256,512]{1,0:T(8,128)(2,1)S(1)}, bf16[256,512]{1,0:T(8,128)(2,1)S(1)}, u32[]{:S(2)}, u32[]{:S(2)}) collective-permute-start(bf16[256,512]{1,0:T(8,128)(2,1)S(1)} %collective-permute-done.12.a3), channel_id=1, source_target_pairs={{0,4},{4,0},{1,5},{5,1},{2,6},{6,2},{3,7},{7,3},{8,12},{12,8},{9,1... | collective-permute-start | bytes 786440 | tf_op jit(solution)/shard_map/ppermute | solution.py:31
  30.2 17.1 %collective-permute-start.14 = (bf16[256,512]{1,0:T(8,128)(2,1)S(1)}, bf16[256,512]{1,0:T(8,128)(2,1)S(1)}, u32[]{:S(2)}, u32[]{:S(2)}) collective-permute-start(bf16[256,512]{1,0:T(8,128)(2,1)S(1)} %collective-permute-done.11.a2), channel_id=1, source_target_pairs={{0,4},{4,0},{1,5},{5,1},{2,6},{6,2},{3,7},{7,3},{8,12},{12,8},{9,1... | collective-permute-start | bytes 786440 | tf_op jit(solution)/shard_map/ppermute | solution.py:31
  30.8 16.5 %collective-permute-start.13 = (bf16[256,512]{1,0:T(8,128)(2,1)S(1)}, bf16[256,512]{1,0:T(8,128)(2,1)S(1)}, u32[]{:S(2)}, u32[]{:S(2)}) collective-permute-start(bf16[256,512]{1,0:T(8,128)(2,1)S(1)} %collective-permute-done.10.a1), channel_id=1, source_target_pairs={{0,4},{4,0},{1,5},{5,1},{2,6},{6,2},{3,7},{7,3},{8,12},{12,8},{9,1... | collective-permute-start | bytes 786440 | tf_op jit(solution)/shard_map/ppermute | solution.py:31
  37.6 14.4 %collective-permute-start.9 = (bf16[512,256]{1,0:T(8,128)(2,1)S(1)}, bf16[512,256]{1,0:T(8,128)(2,1)S(1)}, u32[]{:S(2)}, u32[]{:S(2)}) collective-permute-start(bf16[512,256]{1,0:T(8,128)(2,1)S(1)} %shard_map.120.m0), channel_id=1, source_target_pairs={{0,3},{1,0},{2,1},{3,2},{4,7},{5,4},{6,5},{7,6},{8,11},{9,8},{10,9... | collective-permute-start | bytes 786440 | tf_op jit(solution)/shard_map/ppermute | solution.py:31
  42.0 12.1 %collective-permute-start.8 = (bf16[512,256]{1,0:T(8,128)(2,1)S(1)}, bf16[512,256]{1,0:T(8,128)(2,1)S(1)}, u32[]{:S(2)}, u32[]{:S(2)}) collective-permute-start(bf16[512,256]{1,0:T(8,128)(2,1)S(1)} %shard_map.120.m0), channel_id=1, source_target_pairs={{0,2},{1,3},{2,0},{3,1},{4,6},{5,7},{6,4},{7,5},{8,10},{9,11},{10,... | collective-permute-start | bytes 786440 | tf_op jit(solution)/shard_map/ppermute | solution.py:31
  46.9 11.5 %collective-permute-start.7 = (bf16[512,256]{1,0:T(8,128)(2,1)S(1)}, bf16[512,256]{1,0:T(8,128)(2,1)S(1)}, u32[]{:S(2)}, u32[]{:S(2)}) collective-permute-start(bf16[512,256]{1,0:T(8,128)(2,1)S(1)} %shard_map.120.m0), channel_id=1, source_target_pairs={{0,1},{1,2},{2,3},{3,0},{4,5},{5,6},{6,7},{7,4},{8,9},{9,10},{10,1... | collective-permute-start | bytes 786440 | tf_op jit(solution)/shard_map/ppermute | solution.py:31
  63.9 4.7 %collective-permute-start.22 = (bf16[144,256]{1,0:T(8,128)(2,1)S(1)}, bf16[144,256]{1,0:T(8,128)(2,1)S(1)}, u32[]{:S(2)}, u32[]{:S(2)}) collective-permute-start(bf16[144,256]{1,0:T(8,128)(2,1)S(1)} %add_convert_fusion.2), channel_id=1, source_target_pairs={{0,24},{8,0},{16,8},{24,16},{1,25},{9,1},{17,9},{25,17},{2,26},{10... | collective-permute-start | bytes 221192 | tf_op jit(solution)/shard_map/ppermute | solution.py:31
  65.4 6.5 %collective-permute-start.21 = (bf16[144,256]{1,0:T(8,128)(2,1)S(1)}, bf16[144,256]{1,0:T(8,128)(2,1)S(1)}, u32[]{:S(2)}, u32[]{:S(2)}) collective-permute-start(bf16[144,256]{1,0:T(8,128)(2,1)S(1)} %add_convert_fusion.2), channel_id=1, source_target_pairs={{0,16},{8,24},{16,0},{24,8},{1,17},{9,25},{17,1},{25,9},{2,18},{10... | collective-permute-start | bytes 221192 | tf_op jit(solution)/shard_map/ppermute | solution.py:31
  66.7 6.0 %collective-permute-start.20 = (bf16[144,256]{1,0:T(8,128)(2,1)S(1)}, bf16[144,256]{1,0:T(8,128)(2,1)S(1)}, u32[]{:S(2)}, u32[]{:S(2)}) collective-permute-start(bf16[144,256]{1,0:T(8,128)(2,1)S(1)} %add_convert_fusion.2), channel_id=1, source_target_pairs={{0,8},{8,16},{16,24},{24,0},{1,9},{9,17},{17,25},{25,1},{2,10},{10... | collective-permute-start | bytes 221192 | tf_op jit(solution)/shard_map/ppermute | solution.py:31
  72.8 7.9 %collective-permute-start.23 = (bf16[144,256]{1,0:T(8,128)(2,1)S(1)}, bf16[144,256]{1,0:T(8,128)(2,1)S(1)}, u32[]{:S(2)}, u32[]{:S(2)}) collective-permute-start(bf16[144,256]{1,0:T(8,128)(2,1)S(1)} %add_convert_fusion.1), channel_id=1, source_target_pairs={{0,32},{32,0},{1,33},{33,1},{2,34},{34,2},{3,35},{35,3},{4,36},{36... | collective-permute-start | bytes 221192 | tf_op jit(solution)/shard_map/ppermute | solution.py:31
  74.1 11.7 %collective-permute-start.16 = (bf16[128,256]{1,0:T(8,128)(2,1)S(1)}, bf16[128,256]{1,0:T(8,128)(2,1)S(1)}, u32[]{:S(2)}, u32[]{:S(2)}) collective-permute-start(bf16[128,256]{1,0:T(8,128)(2,1)S(1)} %get-tuple-element.33), channel_id=1, source_target_pairs={{0,64},{64,0},{128,192},{192,128},{1,65},{65,1},{129,193},{193,129... | collective-permute-start | bytes 196616 | tf_op jit(solution)/shard_map/ppermute | solution.py:36
  75.6 11.0 %collective-permute-start.17 = (bf16[128,256]{1,0:T(8,128)(2,1)S(1)}, bf16[128,256]{1,0:T(8,128)(2,1)S(1)}, u32[]{:S(2)}, u32[]{:S(2)}) collective-permute-start(bf16[128,256]{1,0:T(8,128)(2,1)S(1)} %get-tuple-element.34), channel_id=1, source_target_pairs={{0,128},{64,192},{128,0},{192,64},{1,129},{65,193},{129,1},{193,65... | collective-permute-start | bytes 196616 | tf_op jit(solution)/shard_map/ppermute | solution.py:36
  78.4 9.1 %collective-permute-start.18 = (bf16[128,256]{1,0:T(8,128)(2,1)S(1)}, bf16[128,256]{1,0:T(8,128)(2,1)S(1)}, u32[]{:S(2)}, u32[]{:S(2)}) collective-permute-start(bf16[128,256]{1,0:T(8,128)(2,1)S(1)} %get-tuple-element.35), channel_id=1, source_target_pairs={{0,192},{64,128},{128,64},{192,0},{1,193},{65,129},{129,65},{193,1... | collective-permute-start | bytes 196616 | tf_op jit(solution)/shard_map/ppermute | solution.py:36
  80.7 7.4 %collective-permute-start.26 = (bf16[144,256]{1,0:T(8,128)(2,1)S(1)}, bf16[144,256]{1,0:T(8,128)(2,1)S(1)}, u32[]{:S(2)}, u32[]{:S(2)}) collective-permute-start(bf16[144,256]{1,0:T(8,128)(2,1)S(1)} %add_convert_fusion.t0), channel_id=1, source_target_pairs={{0,192},{64,0},{128,64},{192,128},{1,193},{65,1},{129,65},{193,129... | collective-permute-start | bytes 221192 | tf_op jit(solution)/shard_map/ppermute | solution.py:31
  82.7 9.3 %collective-permute-start.25 = (bf16[144,256]{1,0:T(8,128)(2,1)S(1)}, bf16[144,256]{1,0:T(8,128)(2,1)S(1)}, u32[]{:S(2)}, u32[]{:S(2)}) collective-permute-start(bf16[144,256]{1,0:T(8,128)(2,1)S(1)} %add_convert_fusion.t0), channel_id=1, source_target_pairs={{0,128},{64,192},{128,0},{192,64},{1,129},{65,193},{129,1},{193,65... | collective-permute-start | bytes 221192 | tf_op jit(solution)/shard_map/ppermute | solution.py:31
  85.8 7.8 %collective-permute-start.24 = (bf16[144,256]{1,0:T(8,128)(2,1)S(1)}, bf16[144,256]{1,0:T(8,128)(2,1)S(1)}, u32[]{:S(2)}, u32[]{:S(2)}) collective-permute-start(bf16[144,256]{1,0:T(8,128)(2,1)S(1)} %add_convert_fusion.t0), channel_id=1, source_target_pairs={{0,64},{64,128},{128,192},{192,0},{1,65},{65,129},{129,193},{193,1... | collective-permute-start | bytes 221192 | tf_op jit(solution)/shard_map/ppermute | solution.py:31
  95.6 17.1 %collective-permute-start.27 = (bf16[512,256]{1,0:T(8,128)(2,1)S(1)}, bf16[512,256]{1,0:T(8,128)(2,1)S(1)}, u32[]{:S(2)}, u32[]{:S(2)}) collective-permute-start(bf16[512,256]{1,0:T(8,128)(2,1)S(1)} %get-tuple-element.38), channel_id=1, source_target_pairs={{0,1},{1,2},{2,3},{3,0},{4,5},{5,6},{6,7},{7,4},{8,9},{9,10},{10,1... | collective-permute-start | bytes 786440 | tf_op jit(solution)/shard_map/ppermute | solution.py:31
  97.5 15.2 %collective-permute-start.28 = (bf16[512,256]{1,0:T(8,128)(2,1)S(1)}, bf16[512,256]{1,0:T(8,128)(2,1)S(1)}, u32[]{:S(2)}, u32[]{:S(2)}) collective-permute-start(bf16[512,256]{1,0:T(8,128)(2,1)S(1)} %get-tuple-element.39), channel_id=1, source_target_pairs={{0,2},{1,3},{2,0},{3,1},{4,6},{5,7},{6,4},{7,5},{8,10},{9,11},{10,... | collective-permute-start | bytes 786440 | tf_op jit(solution)/shard_map/ppermute | solution.py:31
  97.7 15.0 %collective-permute-start.29 = (bf16[512,256]{1,0:T(8,128)(2,1)S(1)}, bf16[512,256]{1,0:T(8,128)(2,1)S(1)}, u32[]{:S(2)}, u32[]{:S(2)}) collective-permute-start(bf16[512,256]{1,0:T(8,128)(2,1)S(1)} %get-tuple-element.40), channel_id=1, source_target_pairs={{0,3},{1,0},{2,1},{3,2},{4,7},{5,4},{6,5},{7,6},{8,11},{9,8},{10,9... | collective-permute-start | bytes 786440 | tf_op jit(solution)/shard_map/ppermute | solution.py:31
  100.3 6.0 %collective-permute-start.30 = (bf16[128,256]{1,0:T(8,128)(2,1)S(1)}, bf16[128,256]{1,0:T(8,128)(2,1)S(1)}, u32[]{:S(2)}, u32[]{:S(2)}) collective-permute-start(bf16[128,256]{1,0:T(8,128)(2,1)S(1)} %get-tuple-element.42), channel_id=1, source_target_pairs={{0,64},{64,0},{128,192},{192,128},{1,65},{65,1},{129,193},{193,129... | collective-permute-start | bytes 196616 | tf_op jit(solution)/shard_map/ppermute | solution.py:36
  100.5 8.8 %collective-permute-start.31 = (bf16[128,256]{1,0:T(8,128)(2,1)S(1)}, bf16[128,256]{1,0:T(8,128)(2,1)S(1)}, u32[]{:S(2)}, u32[]{:S(2)}) collective-permute-start(bf16[128,256]{1,0:T(8,128)(2,1)S(1)} %get-tuple-element.43), channel_id=1, source_target_pairs={{0,128},{64,192},{128,0},{192,64},{1,129},{65,193},{129,1},{193,65... | collective-permute-start | bytes 196616 | tf_op jit(solution)/shard_map/ppermute | solution.py:36
  106.3 6.4 %collective-permute-start.32 = (bf16[128,256]{1,0:T(8,128)(2,1)S(1)}, bf16[128,256]{1,0:T(8,128)(2,1)S(1)}, u32[]{:S(2)}, u32[]{:S(2)}) collective-permute-start(bf16[128,256]{1,0:T(8,128)(2,1)S(1)} %get-tuple-element.44), channel_id=1, source_target_pairs={{0,192},{64,128},{128,64},{192,0},{1,193},{65,129},{129,65},{193,1... | collective-permute-start | bytes 196616 | tf_op jit(solution)/shard_map/ppermute | solution.py:36
  (10 other events, 251.7 us)
where the time goes:
time: 114 us
  starting transfers between devices  62.1 us (54%)
  waiting for transfers between devices  36 us (32%)
  Pallas kernels  14.1 us (12%)
  other arithmetic  1.6 us (1%)
    ppermute x23, starting transfers between devices, shifted(): lax.ppermute(value, axis, [(i, (i + steps) % count) for i in range(count)])  33.8 us
    ppermute x23, waiting for transfers between devices, shifted(): lax.ppermute(value, axis, [(i, (i + steps) % count) for i in range(count)])  23.6 us
    ppermute x8, starting transfers between devices, flipped(): return lax.ppermute(value, axis, [(i, i ^ mask) for i in range(count)])  20.6 us
    pallas_call x6, Pallas kernels, run(): pl.pallas_call(kernel, in_specs=specs, out_specs=[vmem() for _ in outs],...  14.1 us
    ppermute x8, waiting for transfers between devices, flipped(): return lax.ppermute(value, axis, [(i, i ^ mask) for i in range(count)])  9.27 us
    ppermute x1, starting transfers between devices, body(): after = lax.ppermute(low, nodes_axes, [(j, i) for i, j in up])  5.75 us
  transfers between devices with their start and end apart: 33, of which 16 were waited for; matrix products, arithmetic and copies ran while one was open for 1% of the time, Pallas kernels for 6%

commit v1 on v0

v1 whole, which is shorter than its diff:
```python
import jax
import jax.numpy as jnp
from jax import lax
from jax.experimental import pallas as pl
from jax.experimental.pallas import tpu as pltpu
from jax.sharding import Mesh, PartitionSpec as P

D = 1024
HD = 64
FEAT = 128
BLOCK = 128
HALO_BLK = 2
PEERS = 4
COLS = D // PEERS
EPSILON = 1e-06
SUM_ROWS = 144
F32 = jnp.float32
BF16 = jnp.bfloat16


def vmem():
    return pl.BlockSpec(memory_space=pltpu.VMEM)


def smem():
    return pl.BlockSpec(memory_space=pltpu.SMEM)


def flipped(value, axis, mask):
    count = lax.axis_size(axis)
    return lax.ppermute(value, axis, [(i, i ^ mask) for i in range(count)])


def dot(a, b):
    return jnp.dot(a, b, preferred_element_type=F32)


def dot_t(a, b):
    return lax.dot_general(a, b, (((1,), (1,)), ((), ())), preferred_element_type=F32)


def dot_rows(a, b):
    return lax.dot_general(a, b, (((0,), (0,)), ((), ())), preferred_element_type=F32)


def norm_rows(scaled, part, gain, y):
    for r in range(0, scaled.shape[0], BLOCK):
        places = [pl.multiple_of(lax.bitwise_xor(y, k) * COLS, COLS) for k in range(PEERS)]
        floats = [part(k, r, at) for k, at in enumerate(places)]
        total = sum(jnp.sum(f * f, axis=-1, keepdims=True) for f in floats)
        inverse = lax.rsqrt(total * (1.0 / D) + EPSILON)
        for f, at in zip(floats, places):
            line = gain[:, pl.ds(at, COLS)]
            scaled[r : r + BLOCK, pl.ds(at, COLS)] = (f * inverse * line).astype(BF16)


def fetched(pairs, sems):
    copies = [pltpu.make_async_copy(a, b, sems.at[i]) for i, (a, b) in enumerate(pairs)]
    for copy in copies:
        copy.start()
    for copy in copies:
        copy.wait()


def preload_kernel(c_ref, x_far, gain_far, w_far, out_far, x, gain, w, cut, sems):
    at = pl.multiple_of(c_ref[0] * (D // 2), D // 2)
    part = out_far.at[:, pl.ds(at, D // 2)]
    fetched([(part, cut), (x_far, x), (gain_far, gain), (w_far, w)], sems)


def keys_kernel(y_ref, c_ref, x0, x1, x2, x3, gain, w, inner, outer, scaled):
    parts = (x0, x1, x2, x3)
    norm_rows(scaled, lambda k, r, at: parts[k][r : r + BLOCK, :].astype(F32), gain, y_ref[0])
    half = scaled.shape[0] // 2
    for side, out in ((1 - c_ref[0], inner), (c_ref[0], outer)):
        rows = scaled[pl.ds(pl.multiple_of(side * half, half), half), :]
        for t in (1, 2):
            out[t - 1] = dot(rows, w[t]).astype(BF16)


def head_masks(rows, width):
    lane = lax.broadcasted_iota(jnp.int32, (rows, width), 1)
    return [(lane // HD) == h for h in range(width // HD)]


def stacked_heads(rows, masks):
    rows = rows.astype(F32)
    return jnp.concatenate([jnp.where(m, rows, 0.0).astype(BF16) for m in masks], axis=0)


def picked_heads(stacked, masks):
    picked = stacked[:BLOCK]
    for h in range(1, len(masks)):
        picked = jnp.where(masks[h], stacked[h * BLOCK : (h + 1) * BLOCK], picked)
    return picked


def own_kernel(scaled, w, outer, inner, bias, q, acc, top, totals):
    q[...] = (dot(scaled[...], w[0]).astype(BF16).astype(F32) * HD**-0.5).astype(BF16)
    masks = head_masks(BLOCK, COLS)
    span = outer.shape[1]
    for b in range(q.shape[0] // BLOCK):
        rows = slice(b * BLOCK, (b + 1) * BLOCK)
        stacked = stacked_heads(q[rows, :], masks)
        add = bias[b]
        scores = [
            dot_t(stacked, part[0]) + add[:, j * span : (j + 1) * span]
            for j, part in ((1, outer), (2, inner))
        ]
        best = jnp.max(jnp.maximum(*scores), axis=-1, keepdims=True)
        expo = [jnp.exp(s - best) for s in scores]
        top[b] = jnp.broadcast_to(best, top.shape[1:])
        totals[b] = jnp.broadcast_to(jnp.sum(expo[0] + expo[1], axis=-1, keepdims=True), top.shape[1:])
        mixed = sum(dot(e.astype(BF16), part[1]) for e, part in zip(expo, (outer, inner)))
        acc[rows, :] = picked_heads(mixed, masks)


def merge_kernel(q, outer, inner, bias, acc, top, totals, mixed):
    masks = head_masks(BLOCK, COLS)
    first = masks[0][:, : 2 * HD]
    span = outer.shape[1]

    def spread_heads(rows):
        parts = [rows[h * BLOCK : (h + 1) * BLOCK] for h in range(PEERS)]
        pairs = [jnp.where(first, parts[h], parts[h + 1]) for h in (0, 2)]
        return jnp.concatenate(pairs, axis=1)

    for b in range(q.shape[0] // BLOCK):
        rows = slice(b * BLOCK, (b + 1) * BLOCK)
        stacked = stacked_heads(q[rows, :], masks)
        add = bias[b]
        scores = [
            dot_t(stacked, part[0]) + add[:, j * span : (j + 1) * span]
            for j, part in ((0, outer), (3, inner))
        ]
        seen = top[b]
        best = jnp.maximum(seen, jnp.max(jnp.maximum(*scores), axis=-1, keepdims=True))
        wide = jnp.concatenate([best, best], axis=1)
        expo = [jnp.exp(s - wide) for s in scores]
        keep = jnp.exp(seen - best)
        total = totals[b] * keep + jnp.sum(expo[0] + expo[1], axis=-1, keepdims=True)
        more = sum(dot(e.astype(BF16), part[1]) for e, part in zip(expo, (outer, inner)))
        value = acc[rows, :] * spread_heads(keep) + picked_heads(more, masks)
        mixed[rows, :] = (value / spread_heads(total)).astype(BF16)


def project(y, mixed, w, outs):
    rows = mixed[...]
    for k, out in enumerate(outs):
        at = pl.multiple_of(lax.bitwise_xor(y, k) * COLS, COLS)
        out[...] = dot(rows, w[:, pl.ds(at, COLS)]).astype(BF16).astype(out.dtype)


def spread_features(features, spread):
    spread[...] = jnp.zeros(spread.shape, spread.dtype)
    for h in range(features.shape[0]):
        spread[h * HD : (h + 1) * HD, h * FEAT : (h + 1) * FEAT] = features[h]


def feature_rows(rows, spread):
    angles = dot(rows, spread) * HD**-0.5
    return jnp.where(angles > 0, angles + 1.0, jnp.exp(jnp.minimum(angles, 0.0))).astype(BF16)


def global_kernel(
    y_ref, c_ref, x0, x1, x2, x3, m0, m1, m2, m3, w_own, a1, a2, a3, b1, b2, b3, gain, w, features,
    summary, scaled, hidden, local, spread,
):
    c = c_ref[0]
    wide = D // 2
    for side, given in ((c, (a1, a2, a3)), (1 - c, (b1, b2, b3))):
        at = pl.multiple_of(side * wide, wide)
        out = dot(m0[...], w_own[:, pl.ds(at, wide)])
        for m, part in zip((m1, m2, m3), given):
            out = out + dot(m[...], part[...])
        local[:, pl.ds(at, wide)] = out
    parts = (x0, x1, x2, x3)

    def hidden_rows(k, r, at):
        value = parts[k][r : r + BLOCK, :].astype(F32) + local[r : r + BLOCK, pl.ds(at, COLS)]
        value = value.astype(BF16)
        if k == 0:
            hidden[r : r + BLOCK, :] = value
        return value.astype(F32)

    norm_rows(scaled, hidden_rows, gain, y_ref[0])
    spread_features(features, spread)
    rows = scaled[...]
    gk = dot(rows, w[1]).astype(BF16)
    gv = dot(rows, w[2]).astype(BF16)
    phi = feature_rows(gk, spread[...])
    sums = dot_rows(phi, gv)
    lane = lax.broadcasted_iota(jnp.int32, (FEAT, 2 * HD), 1)
    totals = jnp.sum(phi.astype(F32), axis=0, keepdims=True)
    pads = [jnp.zeros((SUM_ROWS - FEAT - 2, FEAT), F32)]
    halves = []
    for pair in range(2):
        heads = (2 * pair, 2 * pair + 1)
        at = pair * 2 * HD
        left, right = (sums[h * FEAT : (h + 1) * FEAT, at : at + 2 * HD] for h in heads)
        lines = [totals[:, h * FEAT : (h + 1) * FEAT] for h in heads]
        halves.append(jnp.concatenate([jnp.where(lane < HD, left, right), *lines, *pads], axis=0))
    summary[...] = jnp.concatenate(halves, axis=1).astype(BF16)


def queries_kernel(pick, scaled, hidden, w, s0, s1, s2, s3, u0, u1, u2, u3, queries):
    queries[...] = dot(scaled[...], w[0]).astype(BF16)
    for s, (send, keep) in enumerate(((s0, u0), (s1, u1), (s2, u2), (s3, u3))):
        at = pl.multiple_of(pick[s] * BLOCK, BLOCK)
        send[...] = queries[pl.ds(at, BLOCK), :]
        keep[...] = hidden[pl.ds(at, BLOCK), :]


def final_kernel(
    y_ref, place, g0, g1, g2, g3, t0, t1, t2, t3, features, w, own, p1, p2, p3, rows, mixed, spread, table
):
    spread_features(features, spread)
    lane = lax.broadcasted_iota(jnp.int32, (FEAT, 2 * HD), 1)
    table[...] = jnp.zeros(table.shape, table.dtype)
    whole = added(t0[...], t1[...], t2[...], t3[...])
    halves = (whole[:, :FEAT], whole[:, FEAT:])
    for h in range(PEERS):
        half = halves[h // 2]
        at = (h // 2) * 2 * HD
        inside = (lane // HD) == (h % 2)
        line = half[FEAT + h % 2 : FEAT + h % 2 + 1, :]
        column = jnp.transpose(jnp.broadcast_to(line, (FEAT, FEAT)))
        for n, value in enumerate((half[0:FEAT, :], column)):
            spot = (n, slice(h * FEAT, (h + 1) * FEAT), slice(at, at + 2 * HD))
            table[spot] = jnp.where(inside, value, 0.0).astype(BF16)
    for s, got in enumerate((g0, g1, g2, g3)):
        at = pl.multiple_of(place[s] * BLOCK, BLOCK)
        rows[pl.ds(at, BLOCK), :] = got[...]
    phi = feature_rows(rows[...], spread[...])
    numerator = dot(phi, table[0])
    denominator = dot(phi, table[1])
    mixed[...] = (numerator / denominator).astype(BF16)
    project(y_ref[0], mixed, w, (own, p1, p2, p3))


def sum_kernel(place, own, p1, p2, p3, u0, u1, u2, u3, out):
    for s, keep in enumerate((u0, u1, u2, u3)):
        rows = pl.ds(pl.multiple_of(place[s] * BLOCK, BLOCK), BLOCK)
        parts = [part[rows, :].astype(F32) for part in (own, p1, p2, p3)]
        out[rows, :] = (keep[...].astype(F32) + sum(parts)).astype(BF16)


def call(kernel, outs, scratch=(), limit=24, far=()):
    def run(*args):
        specs = [smem() if a.dtype == jnp.int32 else vmem() for a in args]
        args = list(args)
        for i in far:
            specs[i] = pl.BlockSpec(memory_space=pltpu.HBM)
            args[i] = pltpu.with_memory_space_constraint(args[i], pltpu.HBM)
        return pl.pallas_call(
            kernel,
            in_specs=specs,
            out_specs=[vmem() for _ in outs],
            out_shape=[jax.ShapeDtypeStruct(s, d) for s, d in outs],
            scratch_shapes=[s if not isinstance(s, tuple) else pltpu.VMEM(*s) for s in scratch],
            compiler_params=pltpu.CompilerParams(vmem_limit_bytes=limit * 2**20),
        )(*args)

    return run


def added(*parts):
    return sum(p.astype(F32) for p in parts)


def exchanged(pieces, axis):
    got = list(pieces)
    for k in (1, 3, 2):
        got[k] = flipped(pieces[k], axis, k)
    return got


def body(
    nodes_in,
    local_gain,
    qkv,
    local_out,
    global_gain,
    global_qkv,
    global_out,
    feature_map,
    counts,
    neighbours,
    metis,
    hashed,
):
    nodes_axes = ("zq", "zr", "x", "c")
    devices = lax.axis_size(nodes_axes)
    device = lax.axis_index(nodes_axes)
    rows = nodes_in.shape[0]
    blocks = counts.shape[0]
    half = rows // 2
    y = lax.axis_index("y").astype(jnp.int32).reshape(1)
    core = lax.axis_index("c").astype(jnp.int32).reshape(1)
    gains = (local_gain.reshape(1, D), global_gain.reshape(1, D))

    piece = ((rows, COLS), BF16)
    near = exchanged([nodes_in] * PEERS, "y")
    given = (nodes_in, gains[0], qkv, local_out)
    own_x, own_gain, qkv, mine = call(
        preload_kernel,
        [(g.shape, g.dtype) for g in given[:3]] + [((COLS, D // 2), BF16)],
        [pltpu.SemaphoreType.DMA((len(given),))],
        far=(1, 2, 3, 4),
    )(core, *given)
    inputs = [own_x, *near[1:]]
    ids = jnp.stack([metis, hashed])[None]
    ids = jnp.concatenate([ids, flipped(ids, "zq", 1)])
    ids = jnp.concatenate([ids, flipped(ids, "zq", 2)])
    mine = exchanged([mine] * PEERS, "y")[1:]
    other = [flipped(m, "c", 1) for m in mine]
    order = jnp.arange(PEERS, dtype=jnp.int32)

    def where_in(wanted, lists):
        found = jnp.any(lists[:, None, :] == wanted[None, :, None], axis=2)
        return jnp.sum(jnp.where(found, order[None, :], 0), axis=1)

    pick = where_in(metis, ids[:, 1])
    place = where_in(hashed, ids[:, 0])

    window = blocks + 2 * HALO_BLK
    local_index = neighbours - (device * blocks - HALO_BLK)
    turned = (3 - local_index // HALO_BLK) * HALO_BLK + local_index % HALO_BLK
    local_index = jnp.where(core[0] == 0, local_index, turned)
    slots = jnp.arange(neighbours.shape[1], dtype=jnp.int32)
    hits = (local_index[:, :, None] == jnp.arange(window, dtype=jnp.int32)) & (
        slots[None, :, None] < counts[:, None, None]
    )
    times = jnp.sum(hits.astype(F32), axis=1)
    bias = jnp.where(times > 0, jnp.log(jnp.maximum(times, 1.0)), -1e30)
    bias = jnp.repeat(bias, BLOCK, axis=1).reshape(blocks, 1, window * BLOCK)

    pair = (2, half, COLS)
    wide = ((rows, D), BF16)
    inner, outer, scaled = call(keys_kernel, [(pair, BF16), (pair, BF16), wide])(
        y, core, own_x, *inputs[1:], own_gain, qkv
    )
    joined = [(i, i + 1) for i in range(1, devices - 1, 2)]
    joined = joined + [(j, i) for i, j in joined]
    outer_got = lax.ppermute(outer, nodes_axes, joined)
    inner_got = flipped(inner, "c", 1)
    column = ((blocks, PEERS * BLOCK, 2 * HD), F32)
    q, acc, top, totals = call(own_kernel, [piece, ((rows, COLS), F32), column, column])(
        scaled, qkv, outer, inner, bias
    )
    (mixed,) = call(merge_kernel, [piece])(q, outer_got, inner_got, bias, acc, top, totals)
    mixed = exchanged([mixed] * PEERS, "y")

    block = ((BLOCK, COLS), BF16)
    part = ((SUM_ROWS, 2 * FEAT), BF16)
    summary, scaled, hidden = call(
        global_kernel,
        [part, wide, piece],
        [((rows, D), F32), ((COLS, PEERS * FEAT), BF16)],
    )(y, core, own_x, *inputs[1:], *mixed, local_out, *mine, *other, gains[1], global_qkv, feature_map)
    sends = call(queries_kernel, [block] * (2 * PEERS), [piece])(pick, scaled, hidden, global_qkv)

    got, kept = list(sends[:PEERS]), list(sends[PEERS:])
    for k in range(1, PEERS):
        got[k] = flipped(got[k], "zq", k)
        kept[k] = flipped(kept[k], "zq", k)
    summary = added(summary, flipped(summary, "c", 1)).astype(BF16)
    summary = added(summary, flipped(summary, "zr", 1)).astype(BF16)
    summary = added(*exchanged([summary] * PEERS, "x")).astype(BF16)
    parts = exchanged([summary] * PEERS, "zq")

    outs = call(
        final_kernel,
        [piece] * PEERS,
        [piece, piece, ((COLS, PEERS * FEAT), BF16), ((2, PEERS * FEAT, COLS), BF16)],
    )(y, place, *got, *parts, feature_map, global_out)
    outs = exchanged(outs, "y")
    (result,) = call(sum_kernel, [piece])(place, *outs, *kept)
    return result


def solution(mesh):
    fine = Mesh(mesh.devices.reshape(4, 2, 4, 2, 4), ("zq", "zr", "x", "c", "y"))
    n = ("zq", "zr", "x", "c")
    in_specs = (
        P(n, "y"),
        P(),
        P(None, None, "y"),
        P("y", None),
        P(),
        P(None, None, "y"),
        P("y", None),
        P("y", None, None),
        P(n),
        P(n, None),
        P(n),
        P(n),
    )

    def step(*args):
        return body(*args)

    step = jax.shard_map(step, mesh=fine, in_specs=in_specs, out_specs=P(n, "y"), check_vma=False)

    return step
```

time: 114 us -> 109 us (0.956)
  waiting for transfers between devices: 36 us -> 33.2 us
  starting transfers between devices: 62.1 us -> 59.6 us
    ppermute x25 -> x1, starting transfers between devices: 41.5 us -> 1.92 us  [body(): outer_got = lax.ppermute(outer, nodes_axes, joined)]
    ppermute x8 -> x32, starting transfers between devices: 20.6 us -> 57.7 us  [flipped(): return lax.ppermute(value, axis, [(i, i ^ mask) for i in range(count)])]
    ppermute x25 -> x1, waiting for transfers between devices: 26.7 us -> 0.01 us  [body(): outer_got = lax.ppermute(outer, nodes_axes, joined)]
    ppermute x8 -> x32, waiting for transfers between devices: 9.27 us -> 33.2 us  [flipped(): return lax.ppermute(value, axis, [(i, i ^ mask) for i in range(count)])]
    pallas_call x6 -> x8, Pallas kernels: 14.1 us -> 14.7 us  [run(): pl.pallas_call(kernel, in_specs=specs, out_specs=[vmem() for _ in outs],...]
  transfers between devices with their start and end apart: 33 -> 33, of which waited for: 16 -> 12; matrix products, arithmetic and copies ran while one was open for 1% -> 1% of each run, Pallas kernels for 6% -> 7%
where the time goes in v1:
time: 109 us
  starting transfers between devices  59.6 us (55%)
  waiting for transfers between devices  33.2 us (30%)
  Pallas kernels  14.7 us (13%)
    ppermute x32, starting transfers between devices, flipped(): return lax.ppermute(value, axis, [(i, i ^ mask) for i in range(count)])  57.7 us
    ppermute x32, waiting for transfers between devices, flipped(): return lax.ppermute(value, axis, [(i, i ^ mask) for i in range(count)])  33.2 us
    pallas_call x8, Pallas kernels, run(): pl.pallas_call(kernel, in_specs=specs, out_specs=[vmem() for _ in outs],...  14.7 us
  transfers between devices with their start and end apart: 33, of which 12 were waited for; matrix products, arithmetic and copies ran while one was open for 1% of the time, Pallas kernels for 7%

profile of v1, /device:TPU:32, one launch (start us, length us, event | category | flops | bytes accessed | tf_op | source)
XLA Modules:
  0.0 108.8 jit_solution(16740245273974208847)
XLA Ops:
  0.0 1.7 %collective-permute-start.2 = (bf16[512,256]{1,0:T(8,128)(2,1)}, bf16[512,256]{1,0:T(8,128)(2,1)S(1)}, u32[]{:S(2)}, u32[]{:S(2)}) collective-permute-start(bf16[512,256]{1,0:T(8,128)(2,1)} %x_far.1), channel_id=1, source_target_pairs={{0,1},{1,0},{2,3},{3,2},{4,5},{5,4},{6,7},{7,6},{8,9},{9,8},{10,11... | collective-permute-start | bytes 786440 | tf_op jit(solution)/shard_map/ppermute | solution.py:31
  1.7 2.9 %collective-permute-start.3 = (bf16[512,256]{1,0:T(8,128)(2,1)}, bf16[512,256]{1,0:T(8,128)(2,1)S(1)}, u32[]{:S(2)}, u32[]{:S(2)}) collective-permute-start(bf16[512,256]{1,0:T(8,128)(2,1)} %x_far.1), channel_id=1, source_target_pairs={{0,2},{1,3},{2,0},{3,1},{4,6},{5,7},{6,4},{7,5},{8,10},{9,11},{10,... | collective-permute-start | bytes 786440 | tf_op jit(solution)/shard_map/ppermute | solution.py:31
  4.8 1.6 %shard_map.118 = (bf16[512,256]{1,0:T(8,128)(2,1)S(1)}, f32[1,1024]{1,0:T(1,128)S(1)}, bf16[3,1024,256]{2,1,0:T(8,128)(2,1)S(1)}, bf16[256,512]{1,0:T(8,128)(2,1)S(1)}) custom-call(s32[1]{0:T(128)} %bitcast.6.c_ref, bf16[512,256]{1,0:T(8,128)(2,1)} %x_far.1, f32[1,1024]{1,0:T(1,128)} %bitcast.16, bf16[3,1024,256]{2,1,0:T(8,128)(2,1)} %w_far.1, ...), custom_call_target="tpu_custom_call" | custom-call | tf_op jit(solution)/shard_map/pallas_call | solution.py:255
  6.9 4.1 %collective-permute-start.11 = (bf16[256,512]{1,0:T(8,128)(2,1)S(1)}, bf16[256,512]{1,0:T(8,128)(2,1)S(1)}, u32[]{:S(2)}, u32[]{:S(2)}) collective-permute-start(bf16[256,512]{1,0:T(8,128)(2,1)S(1)} %get-tuple-element.41), channel_id=1, source_target_pairs={{0,2},{1,3},{2,0},{3,1},{4,6},{5,7},{6,4},{7,5},{8,10},{9,11},{10,... | collective-permute-start | bytes 786440 | tf_op jit(solution)/shard_map/ppermute | solution.py:31
  12.5 5.1 %collective-permute-done.3.x2 = bf16[512,256]{1,0:T(8,128)(2,1)S(1)} collective-permute-done((bf16[512,256]{1,0:T(8,128)(2,1)}, bf16[512,256]{1,0:T(8,128)(2,1)S(1)}, u32[]{:S(2)}, u32[]{:S(2)}) %collective-permute-start.3) | collective-permute-done | bytes 262176 | tf_op jit(solution)/shard_map/ppermute | solution.py:31
  17.6 3.3 %collective-permute-start = (s32[1,2,4]{2,1,0:T(2,128)S(1)}, s32[1,2,4]{2,1,0:T(2,128)S(1)}, u32[]{:S(2)}, u32[]{:S(2)}) collective-permute-start(s32[1,2,4]{2,1,0:T(2,128)S(1)} %add_bitcast_fusion), channel_id=1, source_target_pairs={{0,64},{64,0},{128,192},{192,128},{1,65},{65,1},{129,193},{193,129... | collective-permute-start | bytes 104 | tf_op jit(solution)/shard_map/ppermute | solution.py:31
  22.1 1.9 %collective-permute-start.5 = (bf16[2,256,256]{2,1,0:T(8,128)(2,1)S(1)}, bf16[2,256,256]{2,1,0:T(8,128)(2,1)S(1)}, u32[]{:S(2)}, u32[]{:S(2)}) collective-permute-start(bf16[2,256,256]{2,1,0:T(8,128)(2,1)S(1)} %get-tuple-element.35.outer), channel_id=1, source_target_pairs={{4,8},{12,16},{20,24},{28,32},{36,40},{44,48},{52,56},{60,64},{68,... | collective-permute-start | bytes 786440 | tf_op jit(solution)/shard_map/ppermute | solution.py:345
  24.0 1.7 %collective-permute-start.6 = (bf16[2,256,256]{2,1,0:T(8,128)(2,1)S(1)}, bf16[2,256,256]{2,1,0:T(8,128)(2,1)S(1)}, u32[]{:S(2)}, u32[]{:S(2)}) collective-permute-start(bf16[2,256,256]{2,1,0:T(8,128)(2,1)S(1)} %get-tuple-element.36.inner), channel_id=1, source_target_pairs={{0,4},{4,0},{1,5},{5,1},{2,6},{6,2},{3,7},{7,3},{8,12},{12,8},{9,1... | collective-permute-start | bytes 786440 | tf_op jit(solution)/shard_map/ppermute | solution.py:31
  25.9 2.2 %shard_map.120 = (bf16[512,256]{1,0:T(8,128)(2,1)S(1)}, f32[512,256]{1,0:T(8,128)S(1)}, f32[4,512,128]{2,1,0:T(8,128)S(1)}, f32[4,512,128]{2,1,0:T(8,128)S(1)}) custom-call(bf16[512,1024]{1,0:T(8,128)(2,1)S(1)} %get-tuple-element.34.scaled, bf16[3,1024,256]{2,1,0:T(8,128)(2,1)S(1)} %get-tuple-element.33.w, bf16[2,256,256]{2,1,0:T(8,128)(2,1)S(1)} %get-tuple-element.35.outer, ...), custom_call_target="tpu_custom_call" | custom-call | tf_op jit(solution)/shard_map/pallas_call | solution.py:255
  28.2 6.3 %collective-permute-start.1 = (s32[2,2,4]{2,1,0:T(2,128)S(1)}, s32[2,2,4]{2,1,0:T(2,128)S(1)}, u32[]{:S(2)}, u32[]{:S(2)}) collective-permute-start(s32[2,2,4]{2,1,0:T(2,128)S(1)} %pad_add_fusion.1), channel_id=1, source_target_pairs={{0,128},{64,192},{128,0},{192,64},{1,129},{65,193},{129,1},{193,65... | collective-permute-start | bytes 200 | tf_op jit(solution)/shard_map/ppermute | solution.py:31
  35.0 2.0 %shard_map.121.m0 = bf16[512,256]{1,0:T(8,128)(2,1)S(1)} custom-call(bf16[512,256]{1,0:T(8,128)(2,1)S(1)} %get-tuple-element.37.q, bf16[2,256,256]{2,1,0:T(8,128)(2,1)S(1)} %collective-permute-done.5.outer, bf16[2,256,256]{2,1,0:T(8,128)(2,1)S(1)} %collective-permute-done.6.inner, f32[4,1,1024]{2,1,0:T(1,128)S(1)} %bitcast.12, ...), custom_call_target="tpu_custom_call" | custom-call | tf_op jit(solution)/shard_map/pallas_call | solution.py:255
  37.3 1.7 %collective-permute-start.8 = (bf16[512,256]{1,0:T(8,128)(2,1)S(1)}, bf16[512,256]{1,0:T(8,128)(2,1)S(1)}, u32[]{:S(2)}, u32[]{:S(2)}) collective-permute-start(bf16[512,256]{1,0:T(8,128)(2,1)S(1)} %shard_map.121.m0), channel_id=1, source_target_pairs={{0,2},{1,3},{2,0},{3,1},{4,6},{5,7},{6,4},{7,5},{8,10},{9,11},{10,... | collective-permute-start | bytes 786440 | tf_op jit(solution)/shard_map/ppermute | solution.py:31
  39.0 3.0 %collective-permute-start.9 = (bf16[512,256]{1,0:T(8,128)(2,1)S(1)}, bf16[512,256]{1,0:T(8,128)(2,1)S(1)}, u32[]{:S(2)}, u32[]{:S(2)}) collective-permute-start(bf16[512,256]{1,0:T(8,128)(2,1)S(1)} %shard_map.121.m0), channel_id=1, source_target_pairs={{0,3},{1,2},{2,1},{3,0},{4,7},{5,6},{6,5},{7,4},{8,11},{9,10},{10,... | collective-permute-start | bytes 786440 | tf_op jit(solution)/shard_map/ppermute | solution.py:31
  42.0 4.4 %collective-permute-done.7.m1 = bf16[512,256]{1,0:T(8,128)(2,1)S(1)} collective-permute-done((bf16[512,256]{1,0:T(8,128)(2,1)S(1)}, bf16[512,256]{1,0:T(8,128)(2,1)S(1)}, u32[]{:S(2)}, u32[]{:S(2)}) %collective-permute-start.7) | collective-permute-done | bytes 262176 | tf_op jit(solution)/shard_map/ppermute | solution.py:31
  46.5 4.5 %collective-permute-done.8.m2 = bf16[512,256]{1,0:T(8,128)(2,1)S(1)} collective-permute-done((bf16[512,256]{1,0:T(8,128)(2,1)S(1)}, bf16[512,256]{1,0:T(8,128)(2,1)S(1)}, u32[]{:S(2)}, u32[]{:S(2)}) %collective-permute-start.8) | collective-permute-done | bytes 262176 | tf_op jit(solution)/shard_map/ppermute | solution.py:31
  51.0 2.7 %collective-permute-done.9.m3 = bf16[512,256]{1,0:T(8,128)(2,1)S(1)} collective-permute-done((bf16[512,256]{1,0:T(8,128)(2,1)S(1)}, bf16[512,256]{1,0:T(8,128)(2,1)S(1)}, u32[]{:S(2)}, u32[]{:S(2)}) %collective-permute-start.9) | collective-permute-done | bytes 262176 | tf_op jit(solution)/shard_map/ppermute | solution.py:31
  53.7 3.5 %shard_map.122 = (bf16[144,256]{1,0:T(8,128)(2,1)S(1)}, bf16[512,1024]{1,0:T(8,128)(2,1)S(1)}, bf16[512,256]{1,0:T(8,128)(2,1)S(1)}) custom-call(s32[1]{0:T(128)} %bitcast.4.y_ref, s32[1]{0:T(128)} %bitcast.6.c_ref, bf16[512,256]{1,0:T(8,128)(2,1)S(1)} %get-tuple-element.31.x0, bf16[512,256]{1,0:T(8,128)(2,1)S(1)} %collective-permute-done.2.x1, ...), custom_call_target="tpu_custom_call" | custom-call | tf_op jit(solution)/shard_map/pallas_call | solution.py:255
  59.8 3.1 %collective-permute-done.20 = bf16[144,256]{1,0:T(8,128)(2,1)S(1)} collective-permute-done((bf16[144,256]{1,0:T(8,128)(2,1)S(1)}, bf16[144,256]{1,0:T(8,128)(2,1)S(1)}, u32[]{:S(2)}, u32[]{:S(2)}) %collective-permute-start.20) | collective-permute-done | bytes 73760 | tf_op jit(solution)/shard_map/ppermute | solution.py:31
  63.0 1.6 %collective-permute-start.21 = (bf16[144,256]{1,0:T(8,128)(2,1)S(1)}, bf16[144,256]{1,0:T(8,128)(2,1)S(1)}, u32[]{:S(2)}, u32[]{:S(2)}) collective-permute-start(bf16[144,256]{1,0:T(8,128)(2,1)S(1)} %add_convert_fusion.1), channel_id=1, source_target_pairs={{0,8},{8,0},{16,24},{24,16},{1,9},{9,1},{17,25},{25,17},{2,10},{10... | collective-permute-start | bytes 221192 | tf_op jit(solution)/shard_map/ppermute | solution.py:31
  64.6 2.3 %collective-permute-start.22 = (bf16[144,256]{1,0:T(8,128)(2,1)S(1)}, bf16[144,256]{1,0:T(8,128)(2,1)S(1)}, u32[]{:S(2)}, u32[]{:S(2)}) collective-permute-start(bf16[144,256]{1,0:T(8,128)(2,1)S(1)} %add_convert_fusion.1), channel_id=1, source_target_pairs={{0,16},{8,24},{16,0},{24,8},{1,17},{9,25},{17,1},{25,9},{2,18},{10... | collective-permute-start | bytes 221192 | tf_op jit(solution)/shard_map/ppermute | solution.py:31
  68.9 1.5 %collective-permute-start.16 = (bf16[128,256]{1,0:T(8,128)(2,1)S(1)}, bf16[128,256]{1,0:T(8,128)(2,1)S(1)}, u32[]{:S(2)}, u32[]{:S(2)}) collective-permute-start(bf16[128,256]{1,0:T(8,128)(2,1)S(1)} %get-tuple-element.45), channel_id=1, source_target_pairs={{0,64},{64,0},{128,192},{192,128},{1,65},{65,1},{129,193},{193,129... | collective-permute-start | bytes 196616 | tf_op jit(solution)/shard_map/ppermute | solution.py:31
  70.5 3.5 %collective-permute-start.17 = (bf16[128,256]{1,0:T(8,128)(2,1)S(1)}, bf16[128,256]{1,0:T(8,128)(2,1)S(1)}, u32[]{:S(2)}, u32[]{:S(2)}) collective-permute-start(bf16[128,256]{1,0:T(8,128)(2,1)S(1)} %get-tuple-element.46), channel_id=1, source_target_pairs={{0,128},{64,192},{128,0},{192,64},{1,129},{65,193},{129,1},{193,65... | collective-permute-start | bytes 196616 | tf_op jit(solution)/shard_map/ppermute | solution.py:31
  74.0 1.5 %collective-permute-start.18 = (bf16[128,256]{1,0:T(8,128)(2,1)S(1)}, bf16[128,256]{1,0:T(8,128)(2,1)S(1)}, u32[]{:S(2)}, u32[]{:S(2)}) collective-permute-start(bf16[128,256]{1,0:T(8,128)(2,1)S(1)} %get-tuple-element.47), channel_id=1, source_target_pairs={{0,192},{64,128},{128,64},{192,0},{1,193},{65,129},{129,65},{193,1... | collective-permute-start | bytes 196616 | tf_op jit(solution)/shard_map/ppermute | solution.py:31
  75.6 1.5 %collective-permute-start.24 = (bf16[144,256]{1,0:T(8,128)(2,1)S(1)}, bf16[144,256]{1,0:T(8,128)(2,1)S(1)}, u32[]{:S(2)}, u32[]{:S(2)}) collective-permute-start(bf16[144,256]{1,0:T(8,128)(2,1)S(1)} %add_convert_fusion.t0), channel_id=1, source_target_pairs={{0,64},{64,0},{128,192},{192,128},{1,65},{65,1},{129,193},{193,129... | collective-permute-start | bytes 221192 | tf_op jit(solution)/shard_map/ppermute | solution.py:31
  77.1 3.5 %collective-permute-start.25 = (bf16[144,256]{1,0:T(8,128)(2,1)S(1)}, bf16[144,256]{1,0:T(8,128)(2,1)S(1)}, u32[]{:S(2)}, u32[]{:S(2)}) collective-permute-start(bf16[144,256]{1,0:T(8,128)(2,1)S(1)} %add_convert_fusion.t0), channel_id=1, source_target_pairs={{0,128},{64,192},{128,0},{192,64},{1,129},{65,193},{129,1},{193,65... | collective-permute-start | bytes 221192 | tf_op jit(solution)/shard_map/ppermute | solution.py:31
  82.7 4.4 %collective-permute-done.25.t2 = bf16[144,256]{1,0:T(8,128)(2,1)S(1)} collective-permute-done((bf16[144,256]{1,0:T(8,128)(2,1)S(1)}, bf16[144,256]{1,0:T(8,128)(2,1)S(1)}, u32[]{:S(2)}, u32[]{:S(2)}) %collective-permute-start.25) | collective-permute-done | bytes 73760 | tf_op jit(solution)/shard_map/ppermute | solution.py:31
  88.2 1.7 %shard_map.124 = (bf16[512,256]{1,0:T(8,128)(2,1)S(1)}, bf16[512,256]{1,0:T(8,128)(2,1)S(1)}, bf16[512,256]{1,0:T(8,128)(2,1)S(1)}, bf16[512,256]{1,0:T(8,128)(2,1)S(1)}) custom-call(s32[1]{0:T(128)} %bitcast.4.y_ref, s32[4]{0:T(128)S(1)} %select_reduce_fusion.1.place, bf16[128,256]{1,0:T(8,128)(2,1)S(1)} %get-tuple-element.44.g0, ...), custom_call_target="tpu_custom_call" | custom-call | tf_op jit(solution)/shard_map/pallas_call | solution.py:255
  90.2 4.4 %collective-permute-start.28 = (bf16[512,256]{1,0:T(8,128)(2,1)S(1)}, bf16[512,256]{1,0:T(8,128)(2,1)S(1)}, u32[]{:S(2)}, u32[]{:S(2)}) collective-permute-start(bf16[512,256]{1,0:T(8,128)(2,1)S(1)} %get-tuple-element.51), channel_id=1, source_target_pairs={{0,2},{1,3},{2,0},{3,1},{4,6},{5,7},{6,4},{7,5},{8,10},{9,11},{10,... | collective-permute-start | bytes 786440 | tf_op jit(solution)/shard_map/ppermute | solution.py:31
  95.7 2.8 %collective-permute-start.31 = (bf16[128,256]{1,0:T(8,128)(2,1)S(1)}, bf16[128,256]{1,0:T(8,128)(2,1)S(1)}, u32[]{:S(2)}, u32[]{:S(2)}) collective-permute-start(bf16[128,256]{1,0:T(8,128)(2,1)S(1)} %get-tuple-element.55), channel_id=1, source_target_pairs={{0,128},{64,192},{128,0},{192,64},{1,129},{65,193},{129,1},{193,65... | collective-permute-start | bytes 196616 | tf_op jit(solution)/shard_map/ppermute | solution.py:31
  98.5 2.0 %collective-permute-done.30.u1 = bf16[128,256]{1,0:T(8,128)(2,1)S(1)} collective-permute-done((bf16[128,256]{1,0:T(8,128)(2,1)S(1)}, bf16[128,256]{1,0:T(8,128)(2,1)S(1)}, u32[]{:S(2)}, u32[]{:S(2)}) %collective-permute-start.30) | collective-permute-done | bytes 65568 | tf_op jit(solution)/shard_map/ppermute | solution.py:31
  100.5 2.5 %collective-permute-start.32 = (bf16[128,256]{1,0:T(8,128)(2,1)S(1)}, bf16[128,256]{1,0:T(8,128)(2,1)S(1)}, u32[]{:S(2)}, u32[]{:S(2)}) collective-permute-start(bf16[128,256]{1,0:T(8,128)(2,1)S(1)} %get-tuple-element.56), channel_id=1, source_target_pairs={{0,192},{64,128},{128,64},{192,0},{1,193},{65,129},{129,65},{193,1... | collective-permute-start | bytes 196616 | tf_op jit(solution)/shard_map/ppermute | solution.py:31
  104.0 3.4 %collective-permute-done.32.u3 = bf16[128,256]{1,0:T(8,128)(2,1)S(1)} collective-permute-done((bf16[128,256]{1,0:T(8,128)(2,1)S(1)}, bf16[128,256]{1,0:T(8,128)(2,1)S(1)}, u32[]{:S(2)}, u32[]{:S(2)}) %collective-permute-start.32) | collective-permute-done | bytes 65568 | tf_op jit(solution)/shard_map/ppermute | solution.py:31
  (76 shorter events, 16.0 us)
Async XLA Ops:
  0.0 11.2 %collective-permute-start.2 = (bf16[512,256]{1,0:T(8,128)(2,1)}, bf16[512,256]{1,0:T(8,128)(2,1)S(1)}, u32[]{:S(2)}, u32[]{:S(2)}) collective-permute-start(bf16[512,256]{1,0:T(8,128)(2,1)} %x_far.1), channel_id=1, source_target_pairs={{0,1},{1,0},{2,3},{3,2},{4,5},{5,4},{6,7},{7,6},{8,9},{9,8},{10,11... | collective-permute-start | bytes 786440 | tf_op jit(solution)/shard_map/ppermute | solution.py:31
  1.7 15.9 %collective-permute-start.3 = (bf16[512,256]{1,0:T(8,128)(2,1)}, bf16[512,256]{1,0:T(8,128)(2,1)S(1)}, u32[]{:S(2)}, u32[]{:S(2)}) collective-permute-start(bf16[512,256]{1,0:T(8,128)(2,1)} %x_far.1), channel_id=1, source_target_pairs={{0,2},{1,3},{2,0},{3,1},{4,6},{5,7},{6,4},{7,5},{8,10},{9,11},{10,... | collective-permute-start | bytes 786440 | tf_op jit(solution)/shard_map/ppermute | solution.py:31
  4.6 16.3 %collective-permute-start.4 = (bf16[512,256]{1,0:T(8,128)(2,1)}, bf16[512,256]{1,0:T(8,128)(2,1)S(1)}, u32[]{:S(2)}, u32[]{:S(2)}) collective-permute-start(bf16[512,256]{1,0:T(8,128)(2,1)} %x_far.1), channel_id=1, source_target_pairs={{0,3},{1,2},{2,1},{3,0},{4,7},{5,6},{6,5},{7,4},{8,11},{9,10},{10,... | collective-permute-start | bytes 786440 | tf_op jit(solution)/shard_map/ppermute | solution.py:31
  6.4 19.3 %collective-permute-start.10 = (bf16[256,512]{1,0:T(8,128)(2,1)S(1)}, bf16[256,512]{1,0:T(8,128)(2,1)S(1)}, u32[]{:S(2)}, u32[]{:S(2)}) collective-permute-start(bf16[256,512]{1,0:T(8,128)(2,1)S(1)} %get-tuple-element.41), channel_id=1, source_target_pairs={{0,1},{1,0},{2,3},{3,2},{4,5},{5,4},{6,7},{7,6},{8,9},{9,8},{10,11... | collective-permute-start | bytes 786440 | tf_op jit(solution)/shard_map/ppermute | solution.py:31
  6.9 21.3 %collective-permute-start.11 = (bf16[256,512]{1,0:T(8,128)(2,1)S(1)}, bf16[256,512]{1,0:T(8,128)(2,1)S(1)}, u32[]{:S(2)}, u32[]{:S(2)}) collective-permute-start(bf16[256,512]{1,0:T(8,128)(2,1)S(1)} %get-tuple-element.41), channel_id=1, source_target_pairs={{0,2},{1,3},{2,0},{3,1},{4,6},{5,7},{6,4},{7,5},{8,10},{9,11},{10,... | collective-permute-start | bytes 786440 | tf_op jit(solution)/shard_map/ppermute | solution.py:31
  11.2 23.3 %collective-permute-start.12 = (bf16[256,512]{1,0:T(8,128)(2,1)S(1)}, bf16[256,512]{1,0:T(8,128)(2,1)S(1)}, u32[]{:S(2)}, u32[]{:S(2)}) collective-permute-start(bf16[256,512]{1,0:T(8,128)(2,1)S(1)} %get-tuple-element.41), channel_id=1, source_target_pairs={{0,3},{1,2},{2,1},{3,0},{4,7},{5,6},{6,5},{7,4},{8,11},{9,10},{10,... | collective-permute-start | bytes 786440 | tf_op jit(solution)/shard_map/ppermute | solution.py:31
  17.6 6.4 %collective-permute-start = (s32[1,2,4]{2,1,0:T(2,128)S(1)}, s32[1,2,4]{2,1,0:T(2,128)S(1)}, u32[]{:S(2)}, u32[]{:S(2)}) collective-permute-start(s32[1,2,4]{2,1,0:T(2,128)S(1)} %add_bitcast_fusion), channel_id=1, source_target_pairs={{0,64},{64,0},{128,192},{192,128},{1,65},{65,1},{129,193},{193,129... | collective-permute-start | bytes 104 | tf_op jit(solution)/shard_map/ppermute | solution.py:31
  22.1 12.5 %collective-permute-start.5 = (bf16[2,256,256]{2,1,0:T(8,128)(2,1)S(1)}, bf16[2,256,256]{2,1,0:T(8,128)(2,1)S(1)}, u32[]{:S(2)}, u32[]{:S(2)}) collective-permute-start(bf16[2,256,256]{2,1,0:T(8,128)(2,1)S(1)} %get-tuple-element.35.outer), channel_id=1, source_target_pairs={{4,8},{12,16},{20,24},{28,32},{36,40},{44,48},{52,56},{60,64},{68,... | collective-permute-start | bytes 786440 | tf_op jit(solution)/shard_map/ppermute | solution.py:345
  24.0 11.0 %collective-permute-start.6 = (bf16[2,256,256]{2,1,0:T(8,128)(2,1)S(1)}, bf16[2,256,256]{2,1,0:T(8,128)(2,1)S(1)}, u32[]{:S(2)}, u32[]{:S(2)}) collective-permute-start(bf16[2,256,256]{2,1,0:T(8,128)(2,1)S(1)} %get-tuple-element.36.inner), channel_id=1, source_target_pairs={{0,4},{4,0},{1,5},{5,1},{2,6},{6,2},{3,7},{7,3},{8,12},{12,8},{9,1... | collective-permute-start | bytes 786440 | tf_op jit(solution)/shard_map/ppermute | solution.py:31
  25.7 13.3 %collective-permute-start.13 = (bf16[256,512]{1,0:T(8,128)(2,1)S(1)}, bf16[256,512]{1,0:T(8,128)(2,1)S(1)}, u32[]{:S(2)}, u32[]{:S(2)}) collective-permute-start(bf16[256,512]{1,0:T(8,128)(2,1)S(1)} %collective-permute-done.10.a1), channel_id=1, source_target_pairs={{0,4},{4,0},{1,5},{5,1},{2,6},{6,2},{3,7},{7,3},{8,12},{12,8},{9,1... | collective-permute-start | bytes 786440 | tf_op jit(solution)/shard_map/ppermute | solution.py:31
  28.2 9.1 %collective-permute-start.1 = (s32[2,2,4]{2,1,0:T(2,128)S(1)}, s32[2,2,4]{2,1,0:T(2,128)S(1)}, u32[]{:S(2)}, u32[]{:S(2)}) collective-permute-start(s32[2,2,4]{2,1,0:T(2,128)S(1)} %pad_add_fusion.1), channel_id=1, source_target_pairs={{0,128},{64,192},{128,0},{192,64},{1,129},{65,193},{129,1},{193,65... | collective-permute-start | bytes 200 | tf_op jit(solution)/shard_map/ppermute | solution.py:31
  34.5 7.5 %collective-permute-start.14 = (bf16[256,512]{1,0:T(8,128)(2,1)S(1)}, bf16[256,512]{1,0:T(8,128)(2,1)S(1)}, u32[]{:S(2)}, u32[]{:S(2)}) collective-permute-start(bf16[256,512]{1,0:T(8,128)(2,1)S(1)} %collective-permute-done.11.a2), channel_id=1, source_target_pairs={{0,4},{4,0},{1,5},{5,1},{2,6},{6,2},{3,7},{7,3},{8,12},{12,8},{9,1... | collective-permute-start | bytes 786440 | tf_op jit(solution)/shard_map/ppermute | solution.py:31
  34.6 7.4 %collective-permute-start.15 = (bf16[256,512]{1,0:T(8,128)(2,1)S(1)}, bf16[256,512]{1,0:T(8,128)(2,1)S(1)}, u32[]{:S(2)}, u32[]{:S(2)}) collective-permute-start(bf16[256,512]{1,0:T(8,128)(2,1)S(1)} %collective-permute-done.12.a3), channel_id=1, source_target_pairs={{0,4},{4,0},{1,5},{5,1},{2,6},{6,2},{3,7},{7,3},{8,12},{12,8},{9,1... | collective-permute-start | bytes 786440 | tf_op jit(solution)/shard_map/ppermute | solution.py:31
  37.0 9.4 %collective-permute-start.7 = (bf16[512,256]{1,0:T(8,128)(2,1)S(1)}, bf16[512,256]{1,0:T(8,128)(2,1)S(1)}, u32[]{:S(2)}, u32[]{:S(2)}) collective-permute-start(bf16[512,256]{1,0:T(8,128)(2,1)S(1)} %shard_map.121.m0), channel_id=1, source_target_pairs={{0,1},{1,0},{2,3},{3,2},{4,5},{5,4},{6,7},{7,6},{8,9},{9,8},{10,11... | collective-permute-start | bytes 786440 | tf_op jit(solution)/shard_map/ppermute | solution.py:31
  37.3 13.7 %collective-permute-start.8 = (bf16[512,256]{1,0:T(8,128)(2,1)S(1)}, bf16[512,256]{1,0:T(8,128)(2,1)S(1)}, u32[]{:S(2)}, u32[]{:S(2)}) collective-permute-start(bf16[512,256]{1,0:T(8,128)(2,1)S(1)} %shard_map.121.m0), channel_id=1, source_target_pairs={{0,2},{1,3},{2,0},{3,1},{4,6},{5,7},{6,4},{7,5},{8,10},{9,11},{10,... | collective-permute-start | bytes 786440 | tf_op jit(solution)/shard_map/ppermute | solution.py:31
  39.0 14.7 %collective-permute-start.9 = (bf16[512,256]{1,0:T(8,128)(2,1)S(1)}, bf16[512,256]{1,0:T(8,128)(2,1)S(1)}, u32[]{:S(2)}, u32[]{:S(2)}) collective-permute-start(bf16[512,256]{1,0:T(8,128)(2,1)S(1)} %shard_map.121.m0), channel_id=1, source_target_pairs={{0,3},{1,2},{2,1},{3,0},{4,7},{5,6},{6,5},{7,4},{8,11},{9,10},{10,... | collective-permute-start | bytes 786440 | tf_op jit(solution)/shard_map/ppermute | solution.py:31
  58.6 4.4 %collective-permute-start.20 = (bf16[144,256]{1,0:T(8,128)(2,1)S(1)}, bf16[144,256]{1,0:T(8,128)(2,1)S(1)}, u32[]{:S(2)}, u32[]{:S(2)}) collective-permute-start(bf16[144,256]{1,0:T(8,128)(2,1)S(1)} %add_convert_fusion.2), channel_id=1, source_target_pairs={{0,32},{32,0},{1,33},{33,1},{2,34},{34,2},{3,35},{35,3},{4,36},{36... | collective-permute-start | bytes 221192 | tf_op jit(solution)/shard_map/ppermute | solution.py:31
  63.0 11.0 %collective-permute-start.21 = (bf16[144,256]{1,0:T(8,128)(2,1)S(1)}, bf16[144,256]{1,0:T(8,128)(2,1)S(1)}, u32[]{:S(2)}, u32[]{:S(2)}) collective-permute-start(bf16[144,256]{1,0:T(8,128)(2,1)S(1)} %add_convert_fusion.1), channel_id=1, source_target_pairs={{0,8},{8,0},{16,24},{24,16},{1,9},{9,1},{17,25},{25,17},{2,10},{10... | collective-permute-start | bytes 221192 | tf_op jit(solution)/shard_map/ppermute | solution.py:31
  64.6 10.9 %collective-permute-start.22 = (bf16[144,256]{1,0:T(8,128)(2,1)S(1)}, bf16[144,256]{1,0:T(8,128)(2,1)S(1)}, u32[]{:S(2)}, u32[]{:S(2)}) collective-permute-start(bf16[144,256]{1,0:T(8,128)(2,1)S(1)} %add_convert_fusion.1), channel_id=1, source_target_pairs={{0,16},{8,24},{16,0},{24,8},{1,17},{9,25},{17,1},{25,9},{2,18},{10... | collective-permute-start | bytes 221192 | tf_op jit(solution)/shard_map/ppermute | solution.py:31
  66.9 8.6 %collective-permute-start.23 = (bf16[144,256]{1,0:T(8,128)(2,1)S(1)}, bf16[144,256]{1,0:T(8,128)(2,1)S(1)}, u32[]{:S(2)}, u32[]{:S(2)}) collective-permute-start(bf16[144,256]{1,0:T(8,128)(2,1)S(1)} %add_convert_fusion.1), channel_id=1, source_target_pairs={{0,24},{8,16},{16,8},{24,0},{1,25},{9,17},{17,9},{25,1},{2,26},{10... | collective-permute-start | bytes 221192 | tf_op jit(solution)/shard_map/ppermute | solution.py:31
  68.9 11.7 %collective-permute-start.16 = (bf16[128,256]{1,0:T(8,128)(2,1)S(1)}, bf16[128,256]{1,0:T(8,128)(2,1)S(1)}, u32[]{:S(2)}, u32[]{:S(2)}) collective-permute-start(bf16[128,256]{1,0:T(8,128)(2,1)S(1)} %get-tuple-element.45), channel_id=1, source_target_pairs={{0,64},{64,0},{128,192},{192,128},{1,65},{65,1},{129,193},{193,129... | collective-permute-start | bytes 196616 | tf_op jit(solution)/shard_map/ppermute | solution.py:31
  70.5 11.8 %collective-permute-start.17 = (bf16[128,256]{1,0:T(8,128)(2,1)S(1)}, bf16[128,256]{1,0:T(8,128)(2,1)S(1)}, u32[]{:S(2)}, u32[]{:S(2)}) collective-permute-start(bf16[128,256]{1,0:T(8,128)(2,1)S(1)} %get-tuple-element.46), channel_id=1, source_target_pairs={{0,128},{64,192},{128,0},{192,64},{1,129},{65,193},{129,1},{193,65... | collective-permute-start | bytes 196616 | tf_op jit(solution)/shard_map/ppermute | solution.py:31
  74.0 8.3 %collective-permute-start.18 = (bf16[128,256]{1,0:T(8,128)(2,1)S(1)}, bf16[128,256]{1,0:T(8,128)(2,1)S(1)}, u32[]{:S(2)}, u32[]{:S(2)}) collective-permute-start(bf16[128,256]{1,0:T(8,128)(2,1)S(1)} %get-tuple-element.47), channel_id=1, source_target_pairs={{0,192},{64,128},{128,64},{192,0},{1,193},{65,129},{129,65},{193,1... | collective-permute-start | bytes 196616 | tf_op jit(solution)/shard_map/ppermute | solution.py:31
  75.6 7.2 %collective-permute-start.24 = (bf16[144,256]{1,0:T(8,128)(2,1)S(1)}, bf16[144,256]{1,0:T(8,128)(2,1)S(1)}, u32[]{:S(2)}, u32[]{:S(2)}) collective-permute-start(bf16[144,256]{1,0:T(8,128)(2,1)S(1)} %add_convert_fusion.t0), channel_id=1, source_target_pairs={{0,64},{64,0},{128,192},{192,128},{1,65},{65,1},{129,193},{193,129... | collective-permute-start | bytes 221192 | tf_op jit(solution)/shard_map/ppermute | solution.py:31
  77.1 10.1 %collective-permute-start.25 = (bf16[144,256]{1,0:T(8,128)(2,1)S(1)}, bf16[144,256]{1,0:T(8,128)(2,1)S(1)}, u32[]{:S(2)}, u32[]{:S(2)}) collective-permute-start(bf16[144,256]{1,0:T(8,128)(2,1)S(1)} %add_convert_fusion.t0), channel_id=1, source_target_pairs={{0,128},{64,192},{128,0},{192,64},{1,129},{65,193},{129,1},{193,65... | collective-permute-start | bytes 221192 | tf_op jit(solution)/shard_map/ppermute | solution.py:31
  80.6 7.6 %collective-permute-start.26 = (bf16[144,256]{1,0:T(8,128)(2,1)S(1)}, bf16[144,256]{1,0:T(8,128)(2,1)S(1)}, u32[]{:S(2)}, u32[]{:S(2)}) collective-permute-start(bf16[144,256]{1,0:T(8,128)(2,1)S(1)} %add_convert_fusion.t0), channel_id=1, source_target_pairs={{0,192},{64,128},{128,64},{192,0},{1,193},{65,129},{129,65},{193,1... | collective-permute-start | bytes 221192 | tf_op jit(solution)/shard_map/ppermute | solution.py:31
  89.9 17.4 %collective-permute-start.27 = (bf16[512,256]{1,0:T(8,128)(2,1)S(1)}, bf16[512,256]{1,0:T(8,128)(2,1)S(1)}, u32[]{:S(2)}, u32[]{:S(2)}) collective-permute-start(bf16[512,256]{1,0:T(8,128)(2,1)S(1)} %get-tuple-element.50), channel_id=1, source_target_pairs={{0,1},{1,0},{2,3},{3,2},{4,5},{5,4},{6,7},{7,6},{8,9},{9,8},{10,11... | collective-permute-start | bytes 786440 | tf_op jit(solution)/shard_map/ppermute | solution.py:31
  90.2 17.1 %collective-permute-start.28 = (bf16[512,256]{1,0:T(8,128)(2,1)S(1)}, bf16[512,256]{1,0:T(8,128)(2,1)S(1)}, u32[]{:S(2)}, u32[]{:S(2)}) collective-permute-start(bf16[512,256]{1,0:T(8,128)(2,1)S(1)} %get-tuple-element.51), channel_id=1, source_target_pairs={{0,2},{1,3},{2,0},{3,1},{4,6},{5,7},{6,4},{7,5},{8,10},{9,11},{10,... | collective-permute-start | bytes 786440 | tf_op jit(solution)/shard_map/ppermute | solution.py:31
  94.6 12.7 %collective-permute-start.29 = (bf16[512,256]{1,0:T(8,128)(2,1)S(1)}, bf16[512,256]{1,0:T(8,128)(2,1)S(1)}, u32[]{:S(2)}, u32[]{:S(2)}) collective-permute-start(bf16[512,256]{1,0:T(8,128)(2,1)S(1)} %get-tuple-element.52), channel_id=1, source_target_pairs={{0,3},{1,2},{2,1},{3,0},{4,7},{5,6},{6,5},{7,4},{8,11},{9,10},{10,... | collective-permute-start | bytes 786440 | tf_op jit(solution)/shard_map/ppermute | solution.py:31
  94.9 5.6 %collective-permute-start.30 = (bf16[128,256]{1,0:T(8,128)(2,1)S(1)}, bf16[128,256]{1,0:T(8,128)(2,1)S(1)}, u32[]{:S(2)}, u32[]{:S(2)}) collective-permute-start(bf16[128,256]{1,0:T(8,128)(2,1)S(1)} %get-tuple-element.54), channel_id=1, source_target_pairs={{0,64},{64,0},{128,192},{192,128},{1,65},{65,1},{129,193},{193,129... | collective-permute-start | bytes 196616 | tf_op jit(solution)/shard_map/ppermute | solution.py:31
  95.7 8.3 %collective-permute-start.31 = (bf16[128,256]{1,0:T(8,128)(2,1)S(1)}, bf16[128,256]{1,0:T(8,128)(2,1)S(1)}, u32[]{:S(2)}, u32[]{:S(2)}) collective-permute-start(bf16[128,256]{1,0:T(8,128)(2,1)S(1)} %get-tuple-element.55), channel_id=1, source_target_pairs={{0,128},{64,192},{128,0},{192,64},{1,129},{65,193},{129,1},{193,65... | collective-permute-start | bytes 196616 | tf_op jit(solution)/shard_map/ppermute | solution.py:31
  100.5 6.9 %collective-permute-start.32 = (bf16[128,256]{1,0:T(8,128)(2,1)S(1)}, bf16[128,256]{1,0:T(8,128)(2,1)S(1)}, u32[]{:S(2)}, u32[]{:S(2)}) collective-permute-start(bf16[128,256]{1,0:T(8,128)(2,1)S(1)} %get-tuple-element.56), channel_id=1, source_target_pairs={{0,192},{64,128},{128,64},{192,0},{1,193},{65,129},{129,65},{193,1... | collective-permute-start | bytes 196616 | tf_op jit(solution)/shard_map/ppermute | solution.py:31
  (10 other events, 140.6 us)

commit v2 on v1

--- a/solution.py
+++ b/solution.py
@@ -68,14 +68,21 @@
     fetched([(part, cut), (x_far, x), (gain_far, gain), (w_far, w)], sems)
 
 
-def keys_kernel(y_ref, c_ref, x0, x1, x2, x3, gain, w, inner, outer, scaled):
+def half_keys(side, scaled, w, out):
+    half = scaled.shape[0] // 2
+    rows = scaled[pl.ds(pl.multiple_of(side * half, half), half), :]
+    for t in (1, 2):
+        out[t - 1] = dot(rows, w[t]).astype(BF16)
+
+
+def keys_kernel(y_ref, c_ref, x0, x1, x2, x3, gain, w, outer, scaled):
     parts = (x0, x1, x2, x3)
     norm_rows(scaled, lambda k, r, at: parts[k][r : r + BLOCK, :].astype(F32), gain, y_ref[0])
-    half = scaled.shape[0] // 2
-    for side, out in ((1 - c_ref[0], inner), (c_ref[0], outer)):
-        rows = scaled[pl.ds(pl.multiple_of(side * half, half), half), :]
-        for t in (1, 2):
-            out[t - 1] = dot(rows, w[t]).astype(BF16)
+    half_keys(c_ref[0], scaled, w, outer)
+
+
+def inner_kernel(c_ref, scaled, w, inner):
+    half_keys(1 - c_ref[0], scaled, w, inner)
 
 
 def head_masks(rows, width):
@@ -337,12 +344,13 @@
 
     pair = (2, half, COLS)
     wide = ((rows, D), BF16)
-    inner, outer, scaled = call(keys_kernel, [(pair, BF16), (pair, BF16), wide])(
+    outer, scaled = call(keys_kernel, [(pair, BF16), wide])(
         y, core, own_x, *inputs[1:], own_gain, qkv
     )
     joined = [(i, i + 1) for i in range(1, devices - 1, 2)]
     joined = joined + [(j, i) for i, j in joined]
     outer_got = lax.ppermute(outer, nodes_axes, joined)
+    (inner,) = call(inner_kernel, [(pair, BF16)])(core, scaled, qkv)
     inner_got = flipped(inner, "c", 1)
     column = ((blocks, PEERS * BLOCK, 2 * HD), F32)
     q, acc, top, totals = call(own_kernel, [piece, ((rows, COLS), F32), column, column])(

time: 109 us -> 111 us (1.018)
  waiting for transfers between devices: 33.2 us -> 35.8 us
  starting transfers between devices: 59.6 us -> 58.4 us
    ppermute x32, starting transfers between devices: 57.7 us -> 54.2 us  [flipped(): return lax.ppermute(value, axis, [(i, i ^ mask) for i in range(count)])]
    ppermute x32, waiting for transfers between devices: 33.2 us -> 35.8 us  [flipped(): return lax.ppermute(value, axis, [(i, i ^ mask) for i in range(count)])]
    ppermute x1, starting transfers between devices: 1.92 us -> 4.24 us  [body(): outer_got = lax.ppermute(outer, nodes_axes, joined)]
    pallas_call x8 -> x9, Pallas kernels: 14.7 us -> 14.8 us  [run(): pl.pallas_call(kernel, in_specs=specs, out_specs=[vmem() for _ in outs],...]
  transfers between devices with their start and end apart: 33 -> 33, of which waited for: 12 -> 13; matrix products, arithmetic and copies ran while one was open for 1% -> 1% of each run, Pallas kernels for 7% -> 7%
where the time goes in v2:
time: 111 us; the launch traced here: 110 us
  starting transfers between devices  58.4 us (53%)
  waiting for transfers between devices  35.8 us (32%)
  Pallas kernels  14.8 us (13%)
    ppermute x32, starting transfers between devices, flipped(): return lax.ppermute(value, axis, [(i, i ^ mask) for i in range(count)])  54.2 us
    ppermute x32, waiting for transfers between devices, flipped(): return lax.ppermute(value, axis, [(i, i ^ mask) for i in range(count)])  35.8 us
    pallas_call x9, Pallas kernels, run(): pl.pallas_call(kernel, in_specs=specs, out_specs=[vmem() for _ in outs],...  14.8 us
    ppermute x1, starting transfers between devices, body(): outer_got = lax.ppermute(outer, nodes_axes, joined)  4.24 us
  transfers between devices with their start and end apart: 33, of which 13 were waited for; matrix products, arithmetic and copies ran while one was open for 1% of the time, Pallas kernels for 7%

profile of v2, /device:TPU:32, one launch (start us, length us, event | category | flops | bytes accessed | tf_op | source)
XLA Modules:
  0.0 110.4 jit_solution(4780914283207717357)
XLA Ops:
  0.0 1.7 %collective-permute-start.2 = (bf16[512,256]{1,0:T(8,128)(2,1)}, bf16[512,256]{1,0:T(8,128)(2,1)S(1)}, u32[]{:S(2)}, u32[]{:S(2)}) collective-permute-start(bf16[512,256]{1,0:T(8,128)(2,1)} %x_far.1), channel_id=1, source_target_pairs={{0,1},{1,0},{2,3},{3,2},{4,5},{5,4},{6,7},{7,6},{8,9},{9,8},{10,11... | collective-permute-start | bytes 786440 | tf_op jit(solution)/shard_map/ppermute | solution.py:31
  1.7 2.9 %collective-permute-start.3 = (bf16[512,256]{1,0:T(8,128)(2,1)}, bf16[512,256]{1,0:T(8,128)(2,1)S(1)}, u32[]{:S(2)}, u32[]{:S(2)}) collective-permute-start(bf16[512,256]{1,0:T(8,128)(2,1)} %x_far.1), channel_id=1, source_target_pairs={{0,2},{1,3},{2,0},{3,1},{4,6},{5,7},{6,4},{7,5},{8,10},{9,11},{10,... | collective-permute-start | bytes 786440 | tf_op jit(solution)/shard_map/ppermute | solution.py:31
  4.8 1.6 %shard_map.118 = (bf16[512,256]{1,0:T(8,128)(2,1)S(1)}, f32[1,1024]{1,0:T(1,128)S(1)}, bf16[3,1024,256]{2,1,0:T(8,128)(2,1)S(1)}, bf16[256,512]{1,0:T(8,128)(2,1)S(1)}) custom-call(s32[1]{0:T(128)} %bitcast.6.c_ref, bf16[512,256]{1,0:T(8,128)(2,1)} %x_far.1, f32[1,1024]{1,0:T(1,128)} %bitcast.16, bf16[3,1024,256]{2,1,0:T(8,128)(2,1)} %w_far.1, ...), custom_call_target="tpu_custom_call" | custom-call | tf_op jit(solution)/shard_map/pallas_call | solution.py:262
  6.9 4.1 %collective-permute-start.11 = (bf16[256,512]{1,0:T(8,128)(2,1)S(1)}, bf16[256,512]{1,0:T(8,128)(2,1)S(1)}, u32[]{:S(2)}, u32[]{:S(2)}) collective-permute-start(bf16[256,512]{1,0:T(8,128)(2,1)S(1)} %get-tuple-element.39), channel_id=1, source_target_pairs={{0,2},{1,3},{2,0},{3,1},{4,6},{5,7},{6,4},{7,5},{8,10},{9,11},{10,... | collective-permute-start | bytes 786440 | tf_op jit(solution)/shard_map/ppermute | solution.py:31
  12.5 5.1 %collective-permute-done.3.x2 = bf16[512,256]{1,0:T(8,128)(2,1)S(1)} collective-permute-done((bf16[512,256]{1,0:T(8,128)(2,1)}, bf16[512,256]{1,0:T(8,128)(2,1)S(1)}, u32[]{:S(2)}, u32[]{:S(2)}) %collective-permute-start.3) | collective-permute-done | bytes 262176 | tf_op jit(solution)/shard_map/ppermute | solution.py:31
  17.6 3.3 %collective-permute-start = (s32[1,2,4]{2,1,0:T(2,128)S(1)}, s32[1,2,4]{2,1,0:T(2,128)S(1)}, u32[]{:S(2)}, u32[]{:S(2)}) collective-permute-start(s32[1,2,4]{2,1,0:T(2,128)S(1)} %add_bitcast_fusion), channel_id=1, source_target_pairs={{0,64},{64,0},{128,192},{192,128},{1,65},{65,1},{129,193},{193,129... | collective-permute-start | bytes 104 | tf_op jit(solution)/shard_map/ppermute | solution.py:31
  22.4 4.2 %collective-permute-start.5 = (bf16[2,256,256]{2,1,0:T(8,128)(2,1)S(1)}, bf16[2,256,256]{2,1,0:T(8,128)(2,1)S(1)}, u32[]{:S(2)}, u32[]{:S(2)}) collective-permute-start(bf16[2,256,256]{2,1,0:T(8,128)(2,1)S(1)} %get-tuple-element.34.outer), channel_id=1, source_target_pairs={{4,8},{12,16},{20,24},{28,32},{36,40},{44,48},{52,56},{60,64},{68,... | collective-permute-start | bytes 786440 | tf_op jit(solution)/shard_map/ppermute | solution.py:352
  26.9 2.2 %shard_map.121 = (bf16[512,256]{1,0:T(8,128)(2,1)S(1)}, f32[512,256]{1,0:T(8,128)S(1)}, f32[4,512,128]{2,1,0:T(8,128)S(1)}, f32[4,512,128]{2,1,0:T(8,128)S(1)}) custom-call(bf16[512,1024]{1,0:T(8,128)(2,1)S(1)} %get-tuple-element.33.scaled, bf16[3,1024,256]{2,1,0:T(8,128)(2,1)S(1)} %get-tuple-element.32.w, bf16[2,256,256]{2,1,0:T(8,128)(2,1)S(1)} %get-tuple-element.34.outer, ...), custom_call_target="tpu_custom_call" | custom-call | tf_op jit(solution)/shard_map/pallas_call | solution.py:262
  29.1 7.2 %collective-permute-start.1 = (s32[2,2,4]{2,1,0:T(2,128)S(1)}, s32[2,2,4]{2,1,0:T(2,128)S(1)}, u32[]{:S(2)}, u32[]{:S(2)}) collective-permute-start(s32[2,2,4]{2,1,0:T(2,128)S(1)} %pad_add_fusion.1), channel_id=1, source_target_pairs={{0,128},{64,192},{128,0},{192,64},{1,129},{65,193},{129,1},{193,65... | collective-permute-start | bytes 200 | tf_op jit(solution)/shard_map/ppermute | solution.py:31
  36.9 2.0 %shard_map.122.m0 = bf16[512,256]{1,0:T(8,128)(2,1)S(1)} custom-call(bf16[512,256]{1,0:T(8,128)(2,1)S(1)} %get-tuple-element.35.q, bf16[2,256,256]{2,1,0:T(8,128)(2,1)S(1)} %collective-permute-done.5.outer, bf16[2,256,256]{2,1,0:T(8,128)(2,1)S(1)} %collective-permute-done.6.inner, f32[4,1,1024]{2,1,0:T(1,128)S(1)} %bitcast.12, ...), custom_call_target="tpu_custom_call" | custom-call | tf_op jit(solution)/shard_map/pallas_call | solution.py:262
  39.2 1.7 %collective-permute-start.8 = (bf16[512,256]{1,0:T(8,128)(2,1)S(1)}, bf16[512,256]{1,0:T(8,128)(2,1)S(1)}, u32[]{:S(2)}, u32[]{:S(2)}) collective-permute-start(bf16[512,256]{1,0:T(8,128)(2,1)S(1)} %shard_map.122.m0), channel_id=1, source_target_pairs={{0,2},{1,3},{2,0},{3,1},{4,6},{5,7},{6,4},{7,5},{8,10},{9,11},{10,... | collective-permute-start | bytes 786440 | tf_op jit(solution)/shard_map/ppermute | solution.py:31
  40.9 3.0 %collective-permute-start.9 = (bf16[512,256]{1,0:T(8,128)(2,1)S(1)}, bf16[512,256]{1,0:T(8,128)(2,1)S(1)}, u32[]{:S(2)}, u32[]{:S(2)}) collective-permute-start(bf16[512,256]{1,0:T(8,128)(2,1)S(1)} %shard_map.122.m0), channel_id=1, source_target_pairs={{0,3},{1,2},{2,1},{3,0},{4,7},{5,6},{6,5},{7,4},{8,11},{9,10},{10,... | collective-permute-start | bytes 786440 | tf_op jit(solution)/shard_map/ppermute | solution.py:31
  43.9 4.4 %collective-permute-done.7.m1 = bf16[512,256]{1,0:T(8,128)(2,1)S(1)} collective-permute-done((bf16[512,256]{1,0:T(8,128)(2,1)S(1)}, bf16[512,256]{1,0:T(8,128)(2,1)S(1)}, u32[]{:S(2)}, u32[]{:S(2)}) %collective-permute-start.7) | collective-permute-done | bytes 262176 | tf_op jit(solution)/shard_map/ppermute | solution.py:31
  48.3 4.6 %collective-permute-done.8.m2 = bf16[512,256]{1,0:T(8,128)(2,1)S(1)} collective-permute-done((bf16[512,256]{1,0:T(8,128)(2,1)S(1)}, bf16[512,256]{1,0:T(8,128)(2,1)S(1)}, u32[]{:S(2)}, u32[]{:S(2)}) %collective-permute-start.8) | collective-permute-done | bytes 262176 | tf_op jit(solution)/shard_map/ppermute | solution.py:31
  53.0 2.7 %collective-permute-done.9.m3 = bf16[512,256]{1,0:T(8,128)(2,1)S(1)} collective-permute-done((bf16[512,256]{1,0:T(8,128)(2,1)S(1)}, bf16[512,256]{1,0:T(8,128)(2,1)S(1)}, u32[]{:S(2)}, u32[]{:S(2)}) %collective-permute-start.9) | collective-permute-done | bytes 262176 | tf_op jit(solution)/shard_map/ppermute | solution.py:31
  55.6 3.5 %shard_map.123 = (bf16[144,256]{1,0:T(8,128)(2,1)S(1)}, bf16[512,1024]{1,0:T(8,128)(2,1)S(1)}, bf16[512,256]{1,0:T(8,128)(2,1)S(1)}) custom-call(s32[1]{0:T(128)} %bitcast.4.y_ref, s32[1]{0:T(128)} %bitcast.6.c_ref, bf16[512,256]{1,0:T(8,128)(2,1)S(1)} %get-tuple-element.30.x0, bf16[512,256]{1,0:T(8,128)(2,1)S(1)} %collective-permute-done.2.x1, ...), custom_call_target="tpu_custom_call" | custom-call | tf_op jit(solution)/shard_map/pallas_call | solution.py:262
  60.9 4.1 %collective-permute-done.20 = bf16[144,256]{1,0:T(8,128)(2,1)S(1)} collective-permute-done((bf16[144,256]{1,0:T(8,128)(2,1)S(1)}, bf16[144,256]{1,0:T(8,128)(2,1)S(1)}, u32[]{:S(2)}, u32[]{:S(2)}) %collective-permute-start.20) | collective-permute-done | bytes 73760 | tf_op jit(solution)/shard_map/ppermute | solution.py:31
  65.1 1.8 %collective-permute-start.22 = (bf16[144,256]{1,0:T(8,128)(2,1)S(1)}, bf16[144,256]{1,0:T(8,128)(2,1)S(1)}, u32[]{:S(2)}, u32[]{:S(2)}) collective-permute-start(bf16[144,256]{1,0:T(8,128)(2,1)S(1)} %add_convert_fusion.1), channel_id=1, source_target_pairs={{0,16},{8,24},{16,0},{24,8},{1,17},{9,25},{17,1},{25,9},{2,18},{10... | collective-permute-start | bytes 221192 | tf_op jit(solution)/shard_map/ppermute | solution.py:31
  66.9 2.9 %collective-permute-start.23 = (bf16[144,256]{1,0:T(8,128)(2,1)S(1)}, bf16[144,256]{1,0:T(8,128)(2,1)S(1)}, u32[]{:S(2)}, u32[]{:S(2)}) collective-permute-start(bf16[144,256]{1,0:T(8,128)(2,1)S(1)} %add_convert_fusion.1), channel_id=1, source_target_pairs={{0,24},{8,16},{16,8},{24,0},{1,25},{9,17},{17,9},{25,1},{2,26},{10... | collective-permute-start | bytes 221192 | tf_op jit(solution)/shard_map/ppermute | solution.py:31
  70.9 1.6 %collective-permute-start.16 = (bf16[128,256]{1,0:T(8,128)(2,1)S(1)}, bf16[128,256]{1,0:T(8,128)(2,1)S(1)}, u32[]{:S(2)}, u32[]{:S(2)}) collective-permute-start(bf16[128,256]{1,0:T(8,128)(2,1)S(1)} %get-tuple-element.43), channel_id=1, source_target_pairs={{0,64},{64,0},{128,192},{192,128},{1,65},{65,1},{129,193},{193,129... | collective-permute-start | bytes 196616 | tf_op jit(solution)/shard_map/ppermute | solution.py:31
  72.4 2.6 %collective-permute-start.17 = (bf16[128,256]{1,0:T(8,128)(2,1)S(1)}, bf16[128,256]{1,0:T(8,128)(2,1)S(1)}, u32[]{:S(2)}, u32[]{:S(2)}) collective-permute-start(bf16[128,256]{1,0:T(8,128)(2,1)S(1)} %get-tuple-element.44), channel_id=1, source_target_pairs={{0,128},{64,192},{128,0},{192,64},{1,129},{65,193},{129,1},{193,65... | collective-permute-start | bytes 196616 | tf_op jit(solution)/shard_map/ppermute | solution.py:31
  75.1 2.4 %collective-permute-start.18 = (bf16[128,256]{1,0:T(8,128)(2,1)S(1)}, bf16[128,256]{1,0:T(8,128)(2,1)S(1)}, u32[]{:S(2)}, u32[]{:S(2)}) collective-permute-start(bf16[128,256]{1,0:T(8,128)(2,1)S(1)} %get-tuple-element.45), channel_id=1, source_target_pairs={{0,192},{64,128},{128,64},{192,0},{1,193},{65,129},{129,65},{193,1... | collective-permute-start | bytes 196616 | tf_op jit(solution)/shard_map/ppermute | solution.py:31
  79.1 2.6 %collective-permute-start.25 = (bf16[144,256]{1,0:T(8,128)(2,1)S(1)}, bf16[144,256]{1,0:T(8,128)(2,1)S(1)}, u32[]{:S(2)}, u32[]{:S(2)}) collective-permute-start(bf16[144,256]{1,0:T(8,128)(2,1)S(1)} %add_convert_fusion.t0), channel_id=1, source_target_pairs={{0,128},{64,192},{128,0},{192,64},{1,129},{65,193},{129,1},{193,65... | collective-permute-start | bytes 221192 | tf_op jit(solution)/shard_map/ppermute | solution.py:31
  81.7 2.4 %collective-permute-start.26 = (bf16[144,256]{1,0:T(8,128)(2,1)S(1)}, bf16[144,256]{1,0:T(8,128)(2,1)S(1)}, u32[]{:S(2)}, u32[]{:S(2)}) collective-permute-start(bf16[144,256]{1,0:T(8,128)(2,1)S(1)} %add_convert_fusion.t0), channel_id=1, source_target_pairs={{0,192},{64,128},{128,64},{192,0},{1,193},{65,129},{129,65},{193,1... | collective-permute-start | bytes 221192 | tf_op jit(solution)/shard_map/ppermute | solution.py:31
  84.2 2.1 %collective-permute-done.18.g3 = bf16[128,256]{1,0:T(8,128)(2,1)S(1)} collective-permute-done((bf16[128,256]{1,0:T(8,128)(2,1)S(1)}, bf16[128,256]{1,0:T(8,128)(2,1)S(1)}, u32[]{:S(2)}, u32[]{:S(2)}) %collective-permute-start.18) | collective-permute-done | bytes 65568 | tf_op jit(solution)/shard_map/ppermute | solution.py:31
  87.5 1.8 %collective-permute-done.26.t3 = bf16[144,256]{1,0:T(8,128)(2,1)S(1)} collective-permute-done((bf16[144,256]{1,0:T(8,128)(2,1)S(1)}, bf16[144,256]{1,0:T(8,128)(2,1)S(1)}, u32[]{:S(2)}, u32[]{:S(2)}) %collective-permute-start.26) | collective-permute-done | bytes 73760 | tf_op jit(solution)/shard_map/ppermute | solution.py:31
  89.4 1.7 %shard_map.125 = (bf16[512,256]{1,0:T(8,128)(2,1)S(1)}, bf16[512,256]{1,0:T(8,128)(2,1)S(1)}, bf16[512,256]{1,0:T(8,128)(2,1)S(1)}, bf16[512,256]{1,0:T(8,128)(2,1)S(1)}) custom-call(s32[1]{0:T(128)} %bitcast.4.y_ref, s32[4]{0:T(128)S(1)} %select_reduce_fusion.1.place, bf16[128,256]{1,0:T(8,128)(2,1)S(1)} %get-tuple-element.42.g0, ...), custom_call_target="tpu_custom_call" | custom-call | tf_op jit(solution)/shard_map/pallas_call | solution.py:262
  91.4 3.5 %collective-permute-start.28 = (bf16[512,256]{1,0:T(8,128)(2,1)S(1)}, bf16[512,256]{1,0:T(8,128)(2,1)S(1)}, u32[]{:S(2)}, u32[]{:S(2)}) collective-permute-start(bf16[512,256]{1,0:T(8,128)(2,1)S(1)} %get-tuple-element.49), channel_id=1, source_target_pairs={{0,2},{1,3},{2,0},{3,1},{4,6},{5,7},{6,4},{7,5},{8,10},{9,11},{10,... | collective-permute-start | bytes 786440 | tf_op jit(solution)/shard_map/ppermute | solution.py:31
  96.9 2.7 %collective-permute-start.31 = (bf16[128,256]{1,0:T(8,128)(2,1)S(1)}, bf16[128,256]{1,0:T(8,128)(2,1)S(1)}, u32[]{:S(2)}, u32[]{:S(2)}) collective-permute-start(bf16[128,256]{1,0:T(8,128)(2,1)S(1)} %get-tuple-element.53), channel_id=1, source_target_pairs={{0,128},{64,192},{128,0},{192,64},{1,129},{65,193},{129,1},{193,65... | collective-permute-start | bytes 196616 | tf_op jit(solution)/shard_map/ppermute | solution.py:31
  99.6 2.3 %collective-permute-done.30.u1 = bf16[128,256]{1,0:T(8,128)(2,1)S(1)} collective-permute-done((bf16[128,256]{1,0:T(8,128)(2,1)S(1)}, bf16[128,256]{1,0:T(8,128)(2,1)S(1)}, u32[]{:S(2)}, u32[]{:S(2)}) %collective-permute-start.30) | collective-permute-done | bytes 65568 | tf_op jit(solution)/shard_map/ppermute | solution.py:31
  102.6 2.5 %collective-permute-done.31.u2 = bf16[128,256]{1,0:T(8,128)(2,1)S(1)} collective-permute-done((bf16[128,256]{1,0:T(8,128)(2,1)S(1)}, bf16[128,256]{1,0:T(8,128)(2,1)S(1)}, u32[]{:S(2)}, u32[]{:S(2)}) %collective-permute-start.31) | collective-permute-done | bytes 65568 | tf_op jit(solution)/shard_map/ppermute | solution.py:31
  105.0 3.9 %collective-permute-done.32.u3 = bf16[128,256]{1,0:T(8,128)(2,1)S(1)} collective-permute-done((bf16[128,256]{1,0:T(8,128)(2,1)S(1)}, bf16[128,256]{1,0:T(8,128)(2,1)S(1)}, u32[]{:S(2)}, u32[]{:S(2)}) %collective-permute-start.32) | collective-permute-done | bytes 65568 | tf_op jit(solution)/shard_map/ppermute | solution.py:31
  (77 shorter events, 15.0 us)
Async XLA Ops:
  0.0 11.2 %collective-permute-start.2 = (bf16[512,256]{1,0:T(8,128)(2,1)}, bf16[512,256]{1,0:T(8,128)(2,1)S(1)}, u32[]{:S(2)}, u32[]{:S(2)}) collective-permute-start(bf16[512,256]{1,0:T(8,128)(2,1)} %x_far.1), channel_id=1, source_target_pairs={{0,1},{1,0},{2,3},{3,2},{4,5},{5,4},{6,7},{7,6},{8,9},{9,8},{10,11... | collective-permute-start | bytes 786440 | tf_op jit(solution)/shard_map/ppermute | solution.py:31
  1.7 15.9 %collective-permute-start.3 = (bf16[512,256]{1,0:T(8,128)(2,1)}, bf16[512,256]{1,0:T(8,128)(2,1)S(1)}, u32[]{:S(2)}, u32[]{:S(2)}) collective-permute-start(bf16[512,256]{1,0:T(8,128)(2,1)} %x_far.1), channel_id=1, source_target_pairs={{0,2},{1,3},{2,0},{3,1},{4,6},{5,7},{6,4},{7,5},{8,10},{9,11},{10,... | collective-permute-start | bytes 786440 | tf_op jit(solution)/shard_map/ppermute | solution.py:31
  4.6 16.3 %collective-permute-start.4 = (bf16[512,256]{1,0:T(8,128)(2,1)}, bf16[512,256]{1,0:T(8,128)(2,1)S(1)}, u32[]{:S(2)}, u32[]{:S(2)}) collective-permute-start(bf16[512,256]{1,0:T(8,128)(2,1)} %x_far.1), channel_id=1, source_target_pairs={{0,3},{1,2},{2,1},{3,0},{4,7},{5,6},{6,5},{7,4},{8,11},{9,10},{10,... | collective-permute-start | bytes 786440 | tf_op jit(solution)/shard_map/ppermute | solution.py:31
  6.4 20.2 %collective-permute-start.10 = (bf16[256,512]{1,0:T(8,128)(2,1)S(1)}, bf16[256,512]{1,0:T(8,128)(2,1)S(1)}, u32[]{:S(2)}, u32[]{:S(2)}) collective-permute-start(bf16[256,512]{1,0:T(8,128)(2,1)S(1)} %get-tuple-element.39), channel_id=1, source_target_pairs={{0,1},{1,0},{2,3},{3,2},{4,5},{5,4},{6,7},{7,6},{8,9},{9,8},{10,11... | collective-permute-start | bytes 786440 | tf_op jit(solution)/shard_map/ppermute | solution.py:31
  6.9 22.2 %collective-permute-start.11 = (bf16[256,512]{1,0:T(8,128)(2,1)S(1)}, bf16[256,512]{1,0:T(8,128)(2,1)S(1)}, u32[]{:S(2)}, u32[]{:S(2)}) collective-permute-start(bf16[256,512]{1,0:T(8,128)(2,1)S(1)} %get-tuple-element.39), channel_id=1, source_target_pairs={{0,2},{1,3},{2,0},{3,1},{4,6},{5,7},{6,4},{7,5},{8,10},{9,11},{10,... | collective-permute-start | bytes 786440 | tf_op jit(solution)/shard_map/ppermute | solution.py:31
  11.2 25.1 %collective-permute-start.12 = (bf16[256,512]{1,0:T(8,128)(2,1)S(1)}, bf16[256,512]{1,0:T(8,128)(2,1)S(1)}, u32[]{:S(2)}, u32[]{:S(2)}) collective-permute-start(bf16[256,512]{1,0:T(8,128)(2,1)S(1)} %get-tuple-element.39), channel_id=1, source_target_pairs={{0,3},{1,2},{2,1},{3,0},{4,7},{5,6},{6,5},{7,4},{8,11},{9,10},{10,... | collective-permute-start | bytes 786440 | tf_op jit(solution)/shard_map/ppermute | solution.py:31
  17.6 4.8 %collective-permute-start = (s32[1,2,4]{2,1,0:T(2,128)S(1)}, s32[1,2,4]{2,1,0:T(2,128)S(1)}, u32[]{:S(2)}, u32[]{:S(2)}) collective-permute-start(s32[1,2,4]{2,1,0:T(2,128)S(1)} %add_bitcast_fusion), channel_id=1, source_target_pairs={{0,64},{64,0},{128,192},{192,128},{1,65},{65,1},{129,193},{193,129... | collective-permute-start | bytes 104 | tf_op jit(solution)/shard_map/ppermute | solution.py:31
  22.3 14.3 %collective-permute-start.6 = (bf16[2,256,256]{2,1,0:T(8,128)(2,1)S(1)}, bf16[2,256,256]{2,1,0:T(8,128)(2,1)S(1)}, u32[]{:S(2)}, u32[]{:S(2)}) collective-permute-start(bf16[2,256,256]{2,1,0:T(8,128)(2,1)S(1)} %shard_map.120.inner), channel_id=1, source_target_pairs={{0,4},{4,0},{1,5},{5,1},{2,6},{6,2},{3,7},{7,3},{8,12},{12,8},{9,1... | collective-permute-start | bytes 786440 | tf_op jit(solution)/shard_map/ppermute | solution.py:31
  22.4 14.4 %collective-permute-start.5 = (bf16[2,256,256]{2,1,0:T(8,128)(2,1)S(1)}, bf16[2,256,256]{2,1,0:T(8,128)(2,1)S(1)}, u32[]{:S(2)}, u32[]{:S(2)}) collective-permute-start(bf16[2,256,256]{2,1,0:T(8,128)(2,1)S(1)} %get-tuple-element.34.outer), channel_id=1, source_target_pairs={{4,8},{12,16},{20,24},{28,32},{36,40},{44,48},{52,56},{60,64},{68,... | collective-permute-start | bytes 786440 | tf_op jit(solution)/shard_map/ppermute | solution.py:352
  26.7 14.2 %collective-permute-start.13 = (bf16[256,512]{1,0:T(8,128)(2,1)S(1)}, bf16[256,512]{1,0:T(8,128)(2,1)S(1)}, u32[]{:S(2)}, u32[]{:S(2)}) collective-permute-start(bf16[256,512]{1,0:T(8,128)(2,1)S(1)} %collective-permute-done.10.a1), channel_id=1, source_target_pairs={{0,4},{4,0},{1,5},{5,1},{2,6},{6,2},{3,7},{7,3},{8,12},{12,8},{9,1... | collective-permute-start | bytes 786440 | tf_op jit(solution)/shard_map/ppermute | solution.py:31
  29.1 10.0 %collective-permute-start.1 = (s32[2,2,4]{2,1,0:T(2,128)S(1)}, s32[2,2,4]{2,1,0:T(2,128)S(1)}, u32[]{:S(2)}, u32[]{:S(2)}) collective-permute-start(s32[2,2,4]{2,1,0:T(2,128)S(1)} %pad_add_fusion.1), channel_id=1, source_target_pairs={{0,128},{64,192},{128,0},{192,64},{1,129},{65,193},{129,1},{193,65... | collective-permute-start | bytes 200 | tf_op jit(solution)/shard_map/ppermute | solution.py:31
  36.4 7.5 %collective-permute-start.14 = (bf16[256,512]{1,0:T(8,128)(2,1)S(1)}, bf16[256,512]{1,0:T(8,128)(2,1)S(1)}, u32[]{:S(2)}, u32[]{:S(2)}) collective-permute-start(bf16[256,512]{1,0:T(8,128)(2,1)S(1)} %collective-permute-done.11.a2), channel_id=1, source_target_pairs={{0,4},{4,0},{1,5},{5,1},{2,6},{6,2},{3,7},{7,3},{8,12},{12,8},{9,1... | collective-permute-start | bytes 786440 | tf_op jit(solution)/shard_map/ppermute | solution.py:31
  36.6 7.3 %collective-permute-start.15 = (bf16[256,512]{1,0:T(8,128)(2,1)S(1)}, bf16[256,512]{1,0:T(8,128)(2,1)S(1)}, u32[]{:S(2)}, u32[]{:S(2)}) collective-permute-start(bf16[256,512]{1,0:T(8,128)(2,1)S(1)} %collective-permute-done.12.a3), channel_id=1, source_target_pairs={{0,4},{4,0},{1,5},{5,1},{2,6},{6,2},{3,7},{7,3},{8,12},{12,8},{9,1... | collective-permute-start | bytes 786440 | tf_op jit(solution)/shard_map/ppermute | solution.py:31
  38.9 9.4 %collective-permute-start.7 = (bf16[512,256]{1,0:T(8,128)(2,1)S(1)}, bf16[512,256]{1,0:T(8,128)(2,1)S(1)}, u32[]{:S(2)}, u32[]{:S(2)}) collective-permute-start(bf16[512,256]{1,0:T(8,128)(2,1)S(1)} %shard_map.122.m0), channel_id=1, source_target_pairs={{0,1},{1,0},{2,3},{3,2},{4,5},{5,4},{6,7},{7,6},{8,9},{9,8},{10,11... | collective-permute-start | bytes 786440 | tf_op jit(solution)/shard_map/ppermute | solution.py:31
  39.2 13.8 %collective-permute-start.8 = (bf16[512,256]{1,0:T(8,128)(2,1)S(1)}, bf16[512,256]{1,0:T(8,128)(2,1)S(1)}, u32[]{:S(2)}, u32[]{:S(2)}) collective-permute-start(bf16[512,256]{1,0:T(8,128)(2,1)S(1)} %shard_map.122.m0), channel_id=1, source_target_pairs={{0,2},{1,3},{2,0},{3,1},{4,6},{5,7},{6,4},{7,5},{8,10},{9,11},{10,... | collective-permute-start | bytes 786440 | tf_op jit(solution)/shard_map/ppermute | solution.py:31
  40.9 14.8 %collective-permute-start.9 = (bf16[512,256]{1,0:T(8,128)(2,1)S(1)}, bf16[512,256]{1,0:T(8,128)(2,1)S(1)}, u32[]{:S(2)}, u32[]{:S(2)}) collective-permute-start(bf16[512,256]{1,0:T(8,128)(2,1)S(1)} %shard_map.122.m0), channel_id=1, source_target_pairs={{0,3},{1,2},{2,1},{3,0},{4,7},{5,6},{6,5},{7,4},{8,11},{9,10},{10,... | collective-permute-start | bytes 786440 | tf_op jit(solution)/shard_map/ppermute | solution.py:31
  60.5 4.4 %collective-permute-start.20 = (bf16[144,256]{1,0:T(8,128)(2,1)S(1)}, bf16[144,256]{1,0:T(8,128)(2,1)S(1)}, u32[]{:S(2)}, u32[]{:S(2)}) collective-permute-start(bf16[144,256]{1,0:T(8,128)(2,1)S(1)} %add_convert_fusion.2), channel_id=1, source_target_pairs={{0,32},{32,0},{1,33},{33,1},{2,34},{34,2},{3,35},{35,3},{4,36},{36... | collective-permute-start | bytes 221192 | tf_op jit(solution)/shard_map/ppermute | solution.py:31
  65.0 10.1 %collective-permute-start.21 = (bf16[144,256]{1,0:T(8,128)(2,1)S(1)}, bf16[144,256]{1,0:T(8,128)(2,1)S(1)}, u32[]{:S(2)}, u32[]{:S(2)}) collective-permute-start(bf16[144,256]{1,0:T(8,128)(2,1)S(1)} %add_convert_fusion.1), channel_id=1, source_target_pairs={{0,8},{8,0},{16,24},{24,16},{1,9},{9,1},{17,25},{25,17},{2,10},{10... | collective-permute-start | bytes 221192 | tf_op jit(solution)/shard_map/ppermute | solution.py:31
  65.1 12.4 %collective-permute-start.22 = (bf16[144,256]{1,0:T(8,128)(2,1)S(1)}, bf16[144,256]{1,0:T(8,128)(2,1)S(1)}, u32[]{:S(2)}, u32[]{:S(2)}) collective-permute-start(bf16[144,256]{1,0:T(8,128)(2,1)S(1)} %add_convert_fusion.1), channel_id=1, source_target_pairs={{0,16},{8,24},{16,0},{24,8},{1,17},{9,25},{17,1},{25,9},{2,18},{10... | collective-permute-start | bytes 221192 | tf_op jit(solution)/shard_map/ppermute | solution.py:31
  66.9 10.6 %collective-permute-start.23 = (bf16[144,256]{1,0:T(8,128)(2,1)S(1)}, bf16[144,256]{1,0:T(8,128)(2,1)S(1)}, u32[]{:S(2)}, u32[]{:S(2)}) collective-permute-start(bf16[144,256]{1,0:T(8,128)(2,1)S(1)} %add_convert_fusion.1), channel_id=1, source_target_pairs={{0,24},{8,16},{16,8},{24,0},{1,25},{9,17},{17,9},{25,1},{2,26},{10... | collective-permute-start | bytes 221192 | tf_op jit(solution)/shard_map/ppermute | solution.py:31
  70.9 10.8 %collective-permute-start.16 = (bf16[128,256]{1,0:T(8,128)(2,1)S(1)}, bf16[128,256]{1,0:T(8,128)(2,1)S(1)}, u32[]{:S(2)}, u32[]{:S(2)}) collective-permute-start(bf16[128,256]{1,0:T(8,128)(2,1)S(1)} %get-tuple-element.43), channel_id=1, source_target_pairs={{0,64},{64,0},{128,192},{192,128},{1,65},{65,1},{129,193},{193,129... | collective-permute-start | bytes 196616 | tf_op jit(solution)/shard_map/ppermute | solution.py:31
  72.4 11.8 %collective-permute-start.17 = (bf16[128,256]{1,0:T(8,128)(2,1)S(1)}, bf16[128,256]{1,0:T(8,128)(2,1)S(1)}, u32[]{:S(2)}, u32[]{:S(2)}) collective-permute-start(bf16[128,256]{1,0:T(8,128)(2,1)S(1)} %get-tuple-element.44), channel_id=1, source_target_pairs={{0,128},{64,192},{128,0},{192,64},{1,129},{65,193},{129,1},{193,65... | collective-permute-start | bytes 196616 | tf_op jit(solution)/shard_map/ppermute | solution.py:31
  75.1 11.3 %collective-permute-start.18 = (bf16[128,256]{1,0:T(8,128)(2,1)S(1)}, bf16[128,256]{1,0:T(8,128)(2,1)S(1)}, u32[]{:S(2)}, u32[]{:S(2)}) collective-permute-start(bf16[128,256]{1,0:T(8,128)(2,1)S(1)} %get-tuple-element.45), channel_id=1, source_target_pairs={{0,192},{64,128},{128,64},{192,0},{1,193},{65,129},{129,65},{193,1... | collective-permute-start | bytes 196616 | tf_op jit(solution)/shard_map/ppermute | solution.py:31
  77.5 8.9 %collective-permute-start.24 = (bf16[144,256]{1,0:T(8,128)(2,1)S(1)}, bf16[144,256]{1,0:T(8,128)(2,1)S(1)}, u32[]{:S(2)}, u32[]{:S(2)}) collective-permute-start(bf16[144,256]{1,0:T(8,128)(2,1)S(1)} %add_convert_fusion.t0), channel_id=1, source_target_pairs={{0,64},{64,0},{128,192},{192,128},{1,65},{65,1},{129,193},{193,129... | collective-permute-start | bytes 221192 | tf_op jit(solution)/shard_map/ppermute | solution.py:31
  79.1 8.4 %collective-permute-start.25 = (bf16[144,256]{1,0:T(8,128)(2,1)S(1)}, bf16[144,256]{1,0:T(8,128)(2,1)S(1)}, u32[]{:S(2)}, u32[]{:S(2)}) collective-permute-start(bf16[144,256]{1,0:T(8,128)(2,1)S(1)} %add_convert_fusion.t0), channel_id=1, source_target_pairs={{0,128},{64,192},{128,0},{192,64},{1,129},{65,193},{129,1},{193,65... | collective-permute-start | bytes 221192 | tf_op jit(solution)/shard_map/ppermute | solution.py:31
  81.7 7.7 %collective-permute-start.26 = (bf16[144,256]{1,0:T(8,128)(2,1)S(1)}, bf16[144,256]{1,0:T(8,128)(2,1)S(1)}, u32[]{:S(2)}, u32[]{:S(2)}) collective-permute-start(bf16[144,256]{1,0:T(8,128)(2,1)S(1)} %add_convert_fusion.t0), channel_id=1, source_target_pairs={{0,192},{64,128},{128,64},{192,0},{1,193},{65,129},{129,65},{193,1... | collective-permute-start | bytes 221192 | tf_op jit(solution)/shard_map/ppermute | solution.py:31
  91.0 17.9 %collective-permute-start.27 = (bf16[512,256]{1,0:T(8,128)(2,1)S(1)}, bf16[512,256]{1,0:T(8,128)(2,1)S(1)}, u32[]{:S(2)}, u32[]{:S(2)}) collective-permute-start(bf16[512,256]{1,0:T(8,128)(2,1)S(1)} %get-tuple-element.48), channel_id=1, source_target_pairs={{0,1},{1,0},{2,3},{3,2},{4,5},{5,4},{6,7},{7,6},{8,9},{9,8},{10,11... | collective-permute-start | bytes 786440 | tf_op jit(solution)/shard_map/ppermute | solution.py:31
  91.4 17.6 %collective-permute-start.28 = (bf16[512,256]{1,0:T(8,128)(2,1)S(1)}, bf16[512,256]{1,0:T(8,128)(2,1)S(1)}, u32[]{:S(2)}, u32[]{:S(2)}) collective-permute-start(bf16[512,256]{1,0:T(8,128)(2,1)S(1)} %get-tuple-element.49), channel_id=1, source_target_pairs={{0,2},{1,3},{2,0},{3,1},{4,6},{5,7},{6,4},{7,5},{8,10},{9,11},{10,... | collective-permute-start | bytes 786440 | tf_op jit(solution)/shard_map/ppermute | solution.py:31
  94.9 14.1 %collective-permute-start.29 = (bf16[512,256]{1,0:T(8,128)(2,1)S(1)}, bf16[512,256]{1,0:T(8,128)(2,1)S(1)}, u32[]{:S(2)}, u32[]{:S(2)}) collective-permute-start(bf16[512,256]{1,0:T(8,128)(2,1)S(1)} %get-tuple-element.50), channel_id=1, source_target_pairs={{0,3},{1,2},{2,1},{3,0},{4,7},{5,6},{6,5},{7,4},{8,11},{9,10},{10,... | collective-permute-start | bytes 786440 | tf_op jit(solution)/shard_map/ppermute | solution.py:31
  96.0 5.9 %collective-permute-start.30 = (bf16[128,256]{1,0:T(8,128)(2,1)S(1)}, bf16[128,256]{1,0:T(8,128)(2,1)S(1)}, u32[]{:S(2)}, u32[]{:S(2)}) collective-permute-start(bf16[128,256]{1,0:T(8,128)(2,1)S(1)} %get-tuple-element.52), channel_id=1, source_target_pairs={{0,64},{64,0},{128,192},{192,128},{1,65},{65,1},{129,193},{193,129... | collective-permute-start | bytes 196616 | tf_op jit(solution)/shard_map/ppermute | solution.py:31
  96.9 8.2 %collective-permute-start.31 = (bf16[128,256]{1,0:T(8,128)(2,1)S(1)}, bf16[128,256]{1,0:T(8,128)(2,1)S(1)}, u32[]{:S(2)}, u32[]{:S(2)}) collective-permute-start(bf16[128,256]{1,0:T(8,128)(2,1)S(1)} %get-tuple-element.53), channel_id=1, source_target_pairs={{0,128},{64,192},{128,0},{192,64},{1,129},{65,193},{129,1},{193,65... | collective-permute-start | bytes 196616 | tf_op jit(solution)/shard_map/ppermute | solution.py:31
  101.9 7.1 %collective-permute-start.32 = (bf16[128,256]{1,0:T(8,128)(2,1)S(1)}, bf16[128,256]{1,0:T(8,128)(2,1)S(1)}, u32[]{:S(2)}, u32[]{:S(2)}) collective-permute-start(bf16[128,256]{1,0:T(8,128)(2,1)S(1)} %get-tuple-element.54), channel_id=1, source_target_pairs={{0,192},{64,128},{128,64},{192,0},{1,193},{65,129},{129,65},{193,1... | collective-permute-start | bytes 196616 | tf_op jit(solution)/shard_map/ppermute | solution.py:31
  (10 other events, 140.0 us)
